TPU v7x, 512 devices: a whole 4x8x8 slice. The times are simulated.
512 devices in a mesh: space: 128 (over y, z, core), tm: 4 (over x).
Axes of the slice: x: 4, y: 8, z: 8, core: 2. Of those that a mesh axis runs over, the one named last changes fastest.
Arguments:
- snapshots: float32 [262144, 1024], P('space', 'tm'), may hold values from -6 to 6
- final_snapshot: float32 [262144], P('space'), may hold values from -6 to 6
- pod_modes: float32 [262144, 200], P('space'), may hold values from -0.01171875 to 0.01171875
- right_vectors: float32 [1024, 200], P('tm'), may hold values from -0.1875 to 0.1875
- inverse_sing: float32 [200], replicated, may hold values from 0.5 to 2
- eigen_vectors: float32 [200, 200], replicated, may hold values from -0.4375 to 0.4375
Outputs:
- reduced_operator: float32 [200, 200], replicated
- dmd_modes: float32 [262144, 200], P(('space', 'tm'))
All inputs are finite; a program needn't handle non-finite values.
Results may differ from a plain program's by a relative error of at most 0.000092.
Values sent between devices are 32-bit elements; how exact they have to be, the bound alone decides.
No kernel may reach another device: no remote copies, remote signals or barrier semaphores. Data moves between devices by JAX's collectives and lax.ppermute only.
A program may use at most 64 MiB of HBM per device.

v0:
```python
import functools

import jax
import jax.numpy as jnp
from jax import lax
from jax.experimental import pallas as pl
from jax.experimental.pallas import tpu as pltpu
from jax.sharding import Mesh
from jax.sharding import PartitionSpec as P

SPACE = ("y_far", "y_near", "z_far", "z_near", "core")
NEAR = ("y_near", "z_near", "core", "tm")
FAR = ("y_far", "z_far")
LANES = 128
CHUNK = 256
VMEM_GRANT = 16 << 20


def f32(*shape):
    return jax.ShapeDtypeStruct(shape, jnp.float32)


def call(kernel, out, *args, smem=0, hbm=(), scratch=()):
    whole = pl.BlockSpec(memory_space=pltpu.VMEM)
    scalar = pl.BlockSpec(memory_space=pltpu.SMEM)
    outs = out if isinstance(out, tuple) else (out,)
    specs = [scalar] * smem + [whole] * (len(args) - smem)
    args = list(args)
    for i in hbm:
        specs[i] = pl.BlockSpec(memory_space=pltpu.HBM)
        args[i] = pltpu.with_memory_space_constraint(args[i], pltpu.HBM)
    result = pl.pallas_call(
        kernel,
        out_shape=outs,
        in_specs=specs,
        scratch_shapes=scratch,
        out_specs=[whole] * len(outs),
        compiler_params=pltpu.CompilerParams(vmem_limit_bytes=VMEM_GRANT),
    )(*args)
    return result if isinstance(out, tuple) else result[0]


def split(x):
    high = x.astype(jnp.bfloat16)
    return high, (x - high.astype(jnp.float32)).astype(jnp.bfloat16)


def three_pass(a, b):
    dims = (((1,), (1,)), ((), ()))
    dot = functools.partial(
        lax.dot_general, dimension_numbers=dims, preferred_element_type=jnp.float32
    )
    (a_high, a_low), (b_high, b_low) = a, b
    return dot(a_high, b_high) + (dot(a_high, b_low) + dot(a_low, b_high))


def products_kernel(
    at_start, snaps, final, modes, vectors, part, term, snaps_in, final_in, modes_in, vectors_in, sems
):
    rank, snapshots = vectors.shape
    rows = part.shape[0]
    chunks = snaps.shape[0] // CHUNK
    spans = [pl.ds(i * CHUNK, CHUNK) for i in range(chunks)]
    got_vectors = pltpu.make_async_copy(vectors, vectors_in, sems.at[2 * chunks])
    got_final = pltpu.make_async_copy(final, final_in, sems.at[2 * chunks + 1])
    got_snaps = [
        pltpu.make_async_copy(snaps.at[here, :], snaps_in.at[here, :], sems.at[i])
        for i, here in enumerate(spans)
    ]
    got_modes = [
        pltpu.make_async_copy(modes.at[:, here], modes_in.at[:, here], sems.at[chunks + i])
        for i, here in enumerate(spans)
    ]
    got_vectors.start()
    got_snaps[0].start()
    got_final.start()
    got_modes[0].start()
    for i in range(1, chunks):
        got_snaps[i].start()
        got_modes[i].start()

    lane = lax.broadcasted_iota(jnp.int32, (rank, snapshots), 1)
    row = lax.broadcasted_iota(jnp.int32, (rows - rank, snapshots), 0)
    column = lax.broadcasted_iota(jnp.int32, (rows - rank, snapshots), 1)
    unit = jnp.where((row == 0) & (column == 0), 1.0, 0.0)
    got_vectors.wait()
    shifted = jnp.where(lane == 0, 0.0, pltpu.roll(vectors_in[...], 1, 1))
    left = split(jnp.concatenate([shifted, unit], axis=0))
    total = None
    for i, here in enumerate(spans):
        got_snaps[i].wait()
        block = three_pass(left, split(snaps_in[here, :]))
        if i == 0:
            got_final.wait()
        below = lax.broadcasted_iota(jnp.int32, block.shape, 0) == rank
        block = jnp.where(below & (at_start[0] == 1), final_in[:, here], block)
        part[:, here] = block
        got_modes[i].wait()
        product = three_pass(split(modes_in[:, here]), split(block))
        total = product if total is None else total + product
    term[...] = total


def packed_kernel(term, before, sing, out):
    rank = before.shape[1]
    rest = rank - LANES
    column = term[:, rank : rank + 1]
    whole = (term[:, :rank] + column * before[...]) * sing[...]
    out[:rank, :] = whole[:, :LANES]
    tail = jnp.pad(whole[:, LANES:], ((0, 2 * LANES - rank), (0, LANES - rest)))
    for i in range(2):
        turned = tail[i * LANES : (i + 1) * LANES].T
        out[rank + i * rest : rank + (i + 1) * rest, :] = turned[:rest]
    out[rank + 2 * rest :, :] = jnp.zeros((out.shape[0] - rank - 2 * rest, LANES), jnp.float32)


def unpacked_kernel(packed, out):
    rank = out.shape[0]
    rest = rank - LANES
    out[:, :LANES] = packed[:rank, :]
    for i, size in ((0, LANES), (1, rest)):
        tail = packed[rank + i * rest : rank + (i + 1) * rest, :]
        turned = jnp.pad(tail, ((0, LANES - rest), (0, 0))).T
        out[i * LANES : i * LANES + size, LANES:] = turned[:size, :rest]


def sum_and_copy_kernel(tiles, out, *, size, copies):
    total = tiles[:size, :]
    for i in range(1, tiles.shape[0] // size):
        total = total + tiles[i * size : (i + 1) * size, :]
    for i in range(copies):
        out[i * size : (i + 1) * size, :] = total


def shares_kernel(me, part, before, to_right, to_left, right_later, left_later, own):
    rank = own.shape[0]
    half = right_later.shape[1]
    turned = jnp.concatenate(
        [
            jnp.broadcast_to(before[:, i * LANES : (i + 1) * LANES], (LANES, LANES)).T
            for i in range(2)
        ],
        axis=0,
    )[:rank, :1]

    def columns(distance, side):
        owner = lax.rem(me[0] + distance, 4)
        here = pl.ds(pl.multiple_of(owner * (2 * half) + side * half, half), half)
        return part[:rank, here] + turned * part[rank : rank + 1, here]

    to_right[:, :half] = columns(2, 0)
    to_right[:, half:] = columns(1, 1)
    to_left[:, :half] = columns(3, 0)
    to_left[:, half:] = columns(2, 1)
    right_later[...] = columns(1, 0)
    left_later[...] = columns(3, 1)
    own[:, :half] = columns(0, 0)
    own[:, half:] = columns(0, 1)


def exchanged(tiles, axes):
    pieces = lax.axis_size(axes)
    got = lax.all_to_all(tiles.reshape(pieces, -1), axes, split_axis=0, concat_axis=0, tiled=True)
    return got.reshape(tiles.shape)


def step(snapshots, final_snapshot, pod_modes, right_vectors, inverse_sing, eigen_vectors):
    blocks = lax.axis_size("tm")
    rows, rank = snapshots.shape[0], right_vectors.shape[1]
    half = rows // (2 * blocks)
    me = lax.axis_index("tm")

    def sent(value, distance):
        return lax.ppermute(value, "tm", [(i, (i + distance) % blocks) for i in range(blocks)])

    before = sent(right_vectors[-1], 1)
    at_start = (me == 0).astype(jnp.int32)[None]
    part, term = call(
        products_kernel,
        (f32(rank + 8, rows), f32(rank, rank + 8)),
        at_start,
        snapshots,
        final_snapshot[None, :],
        pod_modes.T,
        right_vectors.T,
        smem=1,
        hbm=(1, 2, 3, 4),
        scratch=(
            pltpu.VMEM(snapshots.shape, jnp.float32),
            pltpu.VMEM((1, rows), jnp.float32),
            pltpu.VMEM((rank, rows), jnp.float32),
            pltpu.VMEM((rank, snapshots.shape[1]), jnp.float32),
            pltpu.SemaphoreType.DMA((2 * (rows // CHUNK) + 2,)),
        ),
    )

    near, far = lax.axis_size(NEAR), lax.axis_size(FAR)
    size = -(-(rank + 2 * (rank - LANES)) // near)
    packed = call(packed_kernel, f32(near * size, LANES), term, before[None, :], inverse_sing[None, :])
    copied = functools.partial(sum_and_copy_kernel, size=size)
    tiles = exchanged(packed, NEAR)
    tiles = call(functools.partial(copied, copies=far), f32(far * size, LANES), tiles)
    tiles = exchanged(tiles, FAR)
    tiles = call(functools.partial(copied, copies=near), f32(near * size, LANES), tiles)
    tiles = exchanged(tiles, NEAR)
    reduced_operator = call(unpacked_kernel, f32(rank, rank), tiles)

    to_right, to_left, right_later, left_later, own = call(
        shares_kernel,
        (f32(rank, 2 * half), f32(rank, 2 * half), f32(rank, half), f32(rank, half), f32(rank, 2 * half)),
        me.astype(jnp.int32)[None],
        part,
        jnp.pad(before, (0, 2 * LANES - rank))[None, :],
        smem=1,
    )
    from_left = sent(to_right, 1)
    from_right = sent(to_left, -1)
    top = sent(right_later + from_left[:, :half], 1)
    bottom = sent(left_later + from_right[:, half:], -1)
    scaled = own + jnp.concatenate(
        [from_right[:, :half] + top, from_left[:, half:] + bottom], axis=1
    )
    scaled = scaled * inverse_sing[:, None]
    dmd_modes = lax.dot_general(
        eigen_vectors,
        scaled,
        (((0,), (0,)), ((), ())),
        precision=lax.Precision.HIGH,
        preferred_element_type=jnp.float32,
    )
    return reduced_operator, dmd_modes.T


def solution(mesh):
    finer = Mesh(mesh.devices.reshape(4, 2, 4, 2, 2, mesh.shape["tm"]), (*SPACE, "tm"))
    return jax.shard_map(
        step,
        mesh=finer,
        in_specs=(P(SPACE, "tm"), P(SPACE), P(SPACE, None), P("tm", None), P(), P()),
        out_specs=(P(), P((*SPACE, "tm"), None)),
        check_vma=False,
    )
```

profile of v0, /device:TPU:1, one launch (start us, length us, event | category | flops | bytes accessed | tf_op | source)
XLA Modules:
  0.0 84.1 jit_solution(16358282157422958194)
XLA Ops:
  0.6 0.0 copy-start
  0.6 1.1 %slice_reduce_fusion = f32[200]{0:T(256)S(1)} fusion(f32[256,200]{0,1:T(8,128)} %param.9), kind=kLoop, calls=%fused_computation.10 | loop fusion | bytes 1600 | tf_op jit(solution)/shard_map/slice | solution.py:176
  1.8 3.9 %collective-permute-start = (f32[200]{0:T(256)S(1)}, f32[200]{0:T(256)S(1)}, u32[]{:S(2)}, u32[]{:S(2)}) collective-permute-start(f32[200]{0:T(256)S(1)} %slice_reduce_fusion), channel_id=1, source_target_pairs={{0,1},{1,2},{2,3},{3,0},{4,5},{5,6},{6,7},{7,4},{8,9},{9,10},{10,1... | collective-permute-start | bytes 2408 | tf_op jit(solution)/shard_map/ppermute | solution.py:174
  5.7 6.1 %shard_map.77 = (f32[208,2048]{1,0:T(8,128)S(1)}, f32[200,208]{1,0:T(8,128)S(1)}) custom-call(s32[1]{0:T(128)} %bitcast.at_start, f32[2048,256]{1,0:T(8,128)} %snaps.1, f32[1,2048]{1,0:T(1,128)} %bitcast.24, f32[200,2048]{1,0:T(8,128)} %bitcast.22, f32[200,256]{1,0:T(8,128)} %bitcast.23), custom_call_target="tpu_custom_call" | custom-call | tf_op jit(solution)/shard_map/pallas_call | solution.py:32
  11.8 0.0 copy-start.1
  11.8 0.0 collective-permute-done
  11.8 0.3 shard_map.82
  12.1 3.1 %collective-permute-start.2 = (f32[200,512]{1,0:T(8,128)S(1)}, f32[200,512]{1,0:T(8,128)S(1)}, u32[]{:S(2)}, u32[]{:S(2)}) collective-permute-start(f32[200,512]{1,0:T(8,128)S(1)} %get-tuple-element.14), channel_id=1, source_target_pairs={{0,1},{1,2},{2,3},{3,0},{4,5},{5,6},{6,7},{7,4},{8,9},{9,10},{10,1... | collective-permute-start | bytes 1228808 | tf_op jit(solution)/shard_map/ppermute | solution.py:174
  15.2 3.4 %collective-permute-start.1 = (f32[200,512]{1,0:T(8,128)S(1)}, f32[200,512]{1,0:T(8,128)S(1)}, u32[]{:S(2)}, u32[]{:S(2)}) collective-permute-start(f32[200,512]{1,0:T(8,128)S(1)} %get-tuple-element.12), channel_id=1, source_target_pairs={{0,3},{1,0},{2,1},{3,2},{4,7},{5,4},{6,5},{7,6},{8,11},{9,8},{10,9... | collective-permute-start | bytes 1228808 | tf_op jit(solution)/shard_map/ppermute | solution.py:174
  18.6 3.4 %collective-permute-done.2 = f32[200,512]{1,0:T(8,128)S(1)} collective-permute-done((f32[200,512]{1,0:T(8,128)S(1)}, f32[200,512]{1,0:T(8,128)S(1)}, u32[]{:S(2)}, u32[]{:S(2)}) %collective-permute-start.2) | collective-permute-done | bytes 409632 | tf_op jit(solution)/shard_map/ppermute | solution.py:174
  22.0 3.9 %collective-permute-start.3 = (f32[200,256]{1,0:T(8,128)S(1)}, f32[200,256]{1,0:T(8,128)S(1)}, u32[]{:S(2)}, u32[]{:S(2)}) collective-permute-start(f32[200,256]{1,0:T(8,128)S(1)} %slice_add_fusion.2), channel_id=1, source_target_pairs={{0,1},{1,2},{2,3},{3,0},{4,5},{5,6},{6,7},{7,4},{8,9},{9,10},{10,1... | collective-permute-start | bytes 614408 | tf_op jit(solution)/shard_map/ppermute | solution.py:174
  25.9 0.0 copy-done.1
  26.0 0.8 shard_map.78
  26.8 10.6 %all-to-all-start = ((f32[32,1,1408]{2,1,0:T(1,128)}), f32[32,1,1408]{2,1,0:T(1,128)S(1)}, u32[]{:S(2)}, u32[]{:S(2)}) async-start(f32[32,1,1408]{2,1,0:T(1,128)} %bitcast.6), calls=%async_computation | async-start | bytes 360448 | tf_op jit(solution)/shard_map/all_to_all | solution.py:163
  37.4 0.0 collective-permute-done.1
  37.4 0.0 collective-permute-done.3
  37.4 0.1 slice_add_fusion.3
  37.5 4.5 %collective-permute-start.4 = (f32[200,256]{1,0:T(8,128)S(1)}, f32[200,256]{1,0:T(8,128)S(1)}, u32[]{:S(2)}, u32[]{:S(2)}) collective-permute-start(f32[200,256]{1,0:T(8,128)S(1)} %get-tuple-element.17), channel_id=1, source_target_pairs={{0,3},{1,0},{2,1},{3,2},{4,7},{5,4},{6,5},{7,6},{8,11},{9,8},{10,9... | collective-permute-start | bytes 614408 | tf_op jit(solution)/shard_map/ppermute | solution.py:174
  42.0 2.9 %all-to-all-done = f32[32,1,1408]{2,1,0:T(1,128)S(1)} async-done(((f32[32,1,1408]{2,1,0:T(1,128)}), f32[32,1,1408]{2,1,0:T(1,128)S(1)}, u32[]{:S(2)}, u32[]{:S(2)}) %all-to-all-start) | async-done | bytes 180256 | tf_op jit(solution)/shard_map/all_to_all | solution.py:163
  44.8 24.8 %all_to_all.27 = f32[16,1,1408]{2,1,0:T(1,128)S(1)} all-to-all(f32[16,1,1408]{2,1,0:T(1,128)S(1)} %bitcast.17), channel_id=1, replica_groups=mesh['y_far'=4,'y_near'=2,'z_far'=4,'z_near'=2,'core'=2,'tm'=4] {'y_far'..., dimensions={0} | all-to-all | bytes 180224 | tf_op jit(solution)/shard_map/all_to_all | solution.py:163
  69.7 0.7 shard_map.80
  70.4 5.5 %all-to-all-start.2 = ((f32[32,1,1408]{2,1,0:T(1,128)}), f32[32,1,1408]{2,1,0:T(1,128)S(1)}, u32[]{:S(2)}, u32[]{:S(2)}) async-start(f32[32,1,1408]{2,1,0:T(1,128)} %bitcast.10), calls=%async_computation.2 | async-start | bytes 360448 | tf_op jit(solution)/shard_map/all_to_all | solution.py:163
  75.8 0.0 collective-permute-done.4
  75.9 0.0 copy-done
  75.9 1.3 %fusion.1 = f32[512,200]{0,1:T(8,128)} fusion(f32[200,200]{1,0:T(8,128)S(1)} %copy-done, f32[200,512]{1,0:T(8,128)S(1)} %get-tuple-element.11, f32[200,256]{1,0:T(8,128)S(1)} %slice_add_fusion.1, f32[200,256]{1,0:T(8,128)S(1)} %get-tuple-element.16, f32[200]{0:T(256)S(1)} %copy-done.1), kind=kOutput, calls=%fused_computation.2 | convolution fusion | flops 123187200 | bytes 1389600 | tf_op jit(solution)/shard_map/dot_general | solution.py:224
  77.1 6.2 %all-to-all-done.2 = f32[32,1,1408]{2,1,0:T(1,128)S(1)} async-done(((f32[32,1,1408]{2,1,0:T(1,128)}), f32[32,1,1408]{2,1,0:T(1,128)S(1)}, u32[]{:S(2)}, u32[]{:S(2)}) %all-to-all-start.2) | async-done | bytes 180256 | tf_op jit(solution)/shard_map/all_to_all | solution.py:163
  83.3 0.8 shard_map.81
  (4 shorter events, 0.1 us)
Async XLA Ops:
  0.6 75.3 %copy-start = (f32[200,200]{1,0:T(8,128)S(1)}, f32[200,200]{1,0:T(8,128)}, u32[]{:S(2)}) copy-start(f32[200,200]{1,0:T(8,128)} %param.11) | copy-start | bytes 480004
  1.8 10.0 %collective-permute-start = (f32[200]{0:T(256)S(1)}, f32[200]{0:T(256)S(1)}, u32[]{:S(2)}, u32[]{:S(2)}) collective-permute-start(f32[200]{0:T(256)S(1)} %slice_reduce_fusion), channel_id=1, source_target_pairs={{0,1},{1,2},{2,3},{3,0},{4,5},{5,6},{6,7},{7,4},{8,9},{9,10},{10,1... | collective-permute-start | bytes 2408 | tf_op jit(solution)/shard_map/ppermute | solution.py:174
  11.8 14.2 %copy-start.1 = (f32[200]{0:T(256)S(1)}, f32[200]{0:T(256)}, u32[]{:S(2)}) copy-start(f32[200]{0:T(256)} %param.10) | copy-start | bytes 2404
  12.1 9.9 %collective-permute-start.2 = (f32[200,512]{1,0:T(8,128)S(1)}, f32[200,512]{1,0:T(8,128)S(1)}, u32[]{:S(2)}, u32[]{:S(2)}) collective-permute-start(f32[200,512]{1,0:T(8,128)S(1)} %get-tuple-element.14), channel_id=1, source_target_pairs={{0,1},{1,2},{2,3},{3,0},{4,5},{5,6},{6,7},{7,4},{8,9},{9,10},{10,1... | collective-permute-start | bytes 1228808 | tf_op jit(solution)/shard_map/ppermute | solution.py:174
  15.2 22.2 %collective-permute-start.1 = (f32[200,512]{1,0:T(8,128)S(1)}, f32[200,512]{1,0:T(8,128)S(1)}, u32[]{:S(2)}, u32[]{:S(2)}) collective-permute-start(f32[200,512]{1,0:T(8,128)S(1)} %get-tuple-element.12), channel_id=1, source_target_pairs={{0,3},{1,0},{2,1},{3,2},{4,7},{5,4},{6,5},{7,6},{8,11},{9,8},{10,9... | collective-permute-start | bytes 1228808 | tf_op jit(solution)/shard_map/ppermute | solution.py:174
  22.0 15.4 %collective-permute-start.3 = (f32[200,256]{1,0:T(8,128)S(1)}, f32[200,256]{1,0:T(8,128)S(1)}, u32[]{:S(2)}, u32[]{:S(2)}) collective-permute-start(f32[200,256]{1,0:T(8,128)S(1)} %slice_add_fusion.2), channel_id=1, source_target_pairs={{0,1},{1,2},{2,3},{3,0},{4,5},{5,6},{6,7},{7,4},{8,9},{9,10},{10,1... | collective-permute-start | bytes 614408 | tf_op jit(solution)/shard_map/ppermute | solution.py:174
  26.8 18.0 %all-to-all-start = ((f32[32,1,1408]{2,1,0:T(1,128)}), f32[32,1,1408]{2,1,0:T(1,128)S(1)}, u32[]{:S(2)}, u32[]{:S(2)}) async-start(f32[32,1,1408]{2,1,0:T(1,128)} %bitcast.6), calls=%async_computation | async-start | bytes 360448 | tf_op jit(solution)/shard_map/all_to_all | solution.py:163
  37.5 38.4 %collective-permute-start.4 = (f32[200,256]{1,0:T(8,128)S(1)}, f32[200,256]{1,0:T(8,128)S(1)}, u32[]{:S(2)}, u32[]{:S(2)}) collective-permute-start(f32[200,256]{1,0:T(8,128)S(1)} %get-tuple-element.17), channel_id=1, source_target_pairs={{0,3},{1,0},{2,1},{3,2},{4,7},{5,4},{6,5},{7,6},{8,11},{9,8},{10,9... | collective-permute-start | bytes 614408 | tf_op jit(solution)/shard_map/ppermute | solution.py:174
  70.4 13.0 %all-to-all-start.2 = ((f32[32,1,1408]{2,1,0:T(1,128)}), f32[32,1,1408]{2,1,0:T(1,128)S(1)}, u32[]{:S(2)}, u32[]{:S(2)}) async-start(f32[32,1,1408]{2,1,0:T(1,128)} %bitcast.10), calls=%async_computation.2 | async-start | bytes 360448 | tf_op jit(solution)/shard_map/all_to_all | solution.py:163
where the time goes:
time: 84.6 us; the launch traced here: 84.1 us
  starting transfers between devices  34.8 us (41%)
  blocking collectives  24.8 us (29%)
  waiting for transfers between devices  12.5 us (15%)
  Pallas kernels  8.71 us (10%)
  matrix products  1.25 us (1%)
  local copies, waits for them, and re-layouts  1.13 us (1%)
    all_to_all x1, blocking collectives, exchanged(): lax.all_to_all(tiles.reshape(pieces, -1), axes, split_axis=0, concat_axis...  24.8 us
    ppermute x5, starting transfers between devices, sent(): lax.ppermute(value, 'tm', [(i, (i + distance) % blocks) for i in range(bl...  18.8 us
    all_to_all x2, starting transfers between devices, exchanged(): lax.all_to_all(tiles.reshape(pieces, -1), axes, split_axis=0, concat_axis...  16.1 us
    all_to_all x2, waiting for transfers between devices, exchanged(): lax.all_to_all(tiles.reshape(pieces, -1), axes, split_axis=0, concat_axis...  9.05 us
    pallas_call x6, Pallas kernels, call(): pl.pallas_call(kernel, out_shape=outs, in_specs=specs, scratch_shapes=scr...  8.71 us
    ppermute x5, waiting for transfers between devices, sent(): lax.ppermute(value, 'tm', [(i, (i + distance) % blocks) for i in range(bl...  3.41 us
  transfers between devices with their start and end apart: 7, of which 3 were waited for; matrix products, arithmetic and copies ran while one was open for 2% of the time, Pallas kernels for 9%

commit v1 on v0

v1 whole, which is shorter than its diff:
```python
import functools

import jax
import jax.numpy as jnp
from jax import lax
from jax.experimental import pallas as pl
from jax.experimental.pallas import tpu as pltpu
from jax.sharding import Mesh
from jax.sharding import PartitionSpec as P

SPACE = ("y_far", "y_near", "z_far", "z_near", "core")
NEAR = ("y_near", "z_near", "core", "tm")
FAR = ("y_far", "z_far")
LANES = 128
BLOCKS = 4
EXTRA = 2 * BLOCKS
CHUNK = 512
VMEM_GRANT = 16 << 20


def f32(*shape):
    return jax.ShapeDtypeStruct(shape, jnp.float32)


def call(kernel, out, *args, smem=0, hbm=(), scratch=()):
    whole = pl.BlockSpec(memory_space=pltpu.VMEM)
    scalar = pl.BlockSpec(memory_space=pltpu.SMEM)
    outs = out if isinstance(out, tuple) else (out,)
    specs = [scalar] * smem + [whole] * (len(args) - smem)
    args = list(args)
    for i in hbm:
        specs[i] = pl.BlockSpec(memory_space=pltpu.HBM)
        args[i] = pltpu.with_memory_space_constraint(args[i], pltpu.HBM)
    result = pl.pallas_call(
        kernel,
        out_shape=outs,
        in_specs=specs,
        scratch_shapes=scratch,
        out_specs=[whole] * len(outs),
        compiler_params=pltpu.CompilerParams(vmem_limit_bytes=VMEM_GRANT),
    )(*args)
    return result if isinstance(out, tuple) else result[0]


def split(x):
    high = x.astype(jnp.bfloat16)
    return high, (x - high.astype(jnp.float32)).astype(jnp.bfloat16)


def three_pass(a, b, contract=(1, 1)):
    dims = (((contract[0],), (contract[1],)), ((), ()))
    dot = functools.partial(
        lax.dot_general, dimension_numbers=dims, preferred_element_type=jnp.float32
    )
    (a_high, a_low), (b_high, b_low) = a, b
    return dot(a_high, b_high) + (dot(a_high, b_low) + dot(a_low, b_high))


def shifted(vectors):
    lane = lax.broadcasted_iota(jnp.int32, vectors.shape, 1)
    return jnp.where(lane == 0, 0.0, pltpu.roll(vectors, 1, 1))


def turned(row):
    row = jnp.pad(row, ((0, 0), (0, 2 * LANES - row.shape[1])))
    halves = [
        jnp.broadcast_to(row[:, i * LANES : (i + 1) * LANES], (LANES, LANES)).T[:, :1]
        for i in range(2)
    ]
    return jnp.concatenate(halves, axis=0)


def term_kernel(
    me, snaps, final, modes, vectors, packed, snaps_in, final_in, vectors_in, modes_in, sems
):
    rank, _ = vectors.shape
    chunks = snaps.shape[0] // CHUNK
    spans = [pl.ds(i * CHUNK, CHUNK) for i in range(chunks)]
    got_modes = [
        pltpu.make_async_copy(modes.at[:, here], modes_in.at[:, here], sems.at[i])
        for i, here in enumerate(spans)
    ]
    got_snaps = [
        pltpu.make_async_copy(snaps.at[here, :], snaps_in.at[here, :], sems.at[chunks + i])
        for i, here in enumerate(spans)
    ]
    got_final = pltpu.make_async_copy(final, final_in, sems.at[2 * chunks])
    got_vectors = pltpu.make_async_copy(vectors, vectors_in, sems.at[2 * chunks + 1])
    for i in range(chunks):
        got_modes[i].start()
        got_snaps[i].start()
    got_final.start()
    got_vectors.start()

    total = of_final = None
    for i, here in enumerate(spans):
        got_modes[i].wait()
        got_snaps[i].wait()
        left = split(modes_in[:, here])
        product = three_pass(left, split(snaps_in[here, :]), (1, 0))
        if i == 0:
            got_final.wait()
        column = three_pass(left, split(jnp.broadcast_to(final_in[:, here], (8, CHUNK))))
        total = product if total is None else total + product
        of_final = column if of_final is None else of_final + column
    got_vectors.wait()
    whole = three_pass(split(total), split(shifted(vectors_in[...])))
    first = jnp.where(me[0] == 0, of_final[:, :1], total[:, :1])
    packed[:rank, :] = whole[:, :LANES]
    rest = rank - LANES
    tail = jnp.pad(whole[:, LANES:], ((0, 0), (0, LANES - rest)))
    lane = lax.broadcasted_iota(jnp.int32, tail.shape, 1)
    tail = jnp.where(lane == rest + me[0], first, tail)
    tail = jnp.pad(tail, ((0, 2 * LANES - rank), (0, 0)))
    used = rest + BLOCKS
    for i in range(2):
        turn = tail[i * LANES : (i + 1) * LANES].T
        packed[rank + i * used : rank + (i + 1) * used, :] = turn[:used]


def shares_kernel(
    me, snaps, final, vectors, to_right, to_left, right_later, left_later, own
):
    rank, snapshots = vectors.shape
    half = right_later.shape[1]
    row = lax.broadcasted_iota(jnp.int32, (EXTRA, snapshots), 0)
    column = lax.broadcasted_iota(jnp.int32, (EXTRA, snapshots), 1)
    unit = jnp.where((row == me[0]) & (column == 0), 1.0, 0.0)
    left = split(jnp.concatenate([shifted(vectors[...]), unit], axis=0))
    tail = jnp.pad(vectors[:, snapshots - LANES :], ((0, 2 * LANES - rank), (0, 0)))
    last = jnp.concatenate([tail[:LANES].T[LANES - 1 :], tail[LANES:].T[LANES - 1 :]], axis=1)
    slot = lax.broadcasted_iota(jnp.int32, (EXTRA, half), 0)
    after = BLOCKS + lax.rem(me[0] + 1, BLOCKS)

    def write(out, at, distance, side):
        owner = lax.rem(me[0] + distance, BLOCKS)
        here = pl.ds(pl.multiple_of(owner * (2 * half) + side * half, half), half)
        block = three_pass(left, split(snaps[here, :]))
        extra = jnp.where((slot == me[0]) & (me[0] == 0), final[:, here], block[rank:])
        there = slice(at * half, (at + 1) * half)
        out[:rank, there] = block[:rank]
        out[rank:, there] = jnp.where(slot == after, last, extra)

    write(to_right, 0, 2, 0)
    write(to_right, 1, 1, 1)
    write(to_left, 0, 3, 0)
    write(to_left, 1, 2, 1)
    write(right_later, 0, 1, 0)
    write(left_later, 0, 3, 1)
    write(own, 0, 0, 0)
    write(own, 1, 0, 1)


def add_kernel(later, arrived, out, *, side):
    half = out.shape[1]
    out[...] = later[...] + arrived[:, side * half : (side + 1) * half]


def sum_and_copy_kernel(tiles, out, *, size, copies):
    total = tiles[:size, :]
    for i in range(1, tiles.shape[0] // size):
        total = total + tiles[i * size : (i + 1) * size, :]
    for i in range(copies):
        out[i * size : (i + 1) * size, :] = total


def dmd_kernel(own, from_right, from_left, top, bottom, sing, vectors, out, rows):
    rank = out.shape[0]
    half = top.shape[1]
    scale = turned(sing[...])[:rank]
    right = split(vectors[...])
    for i, arrived in ((0, from_right[:, :half] + top[...]), (1, from_left[:, half:] + bottom[...])):
        there = slice(i * half, (i + 1) * half)
        total = own[:, there] + arrived
        first = total[rank : rank + BLOCKS]
        last = total[rank + BLOCKS :, :rank]
        if i == 0:
            rows[...] = last
        summed = total[:rank] + three_pass(split(last), split(first), (0, 0))
        out[:, there] = three_pass(right, split(summed * scale), (0, 0))


def operator_kernel(packed, rows, sing, out):
    rank = out.shape[0]
    rest = rank - LANES
    used = rest + BLOCKS
    first = jnp.concatenate(
        [
            packed[rank + rest : rank + used, :],
            packed[rank + used + rest : rank + 2 * used, :][:, :rest],
        ],
        axis=1,
    )
    term = three_pass(split(first), split(rows[...]), (0, 0))
    scale = sing[...]
    out[:, :LANES] = (packed[:rank, :] + term[:, :LANES]) * scale[:, :LANES]
    for i, size in ((0, LANES), (1, rest)):
        tail = packed[rank + i * used : rank + i * used + rest, :]
        turn = jnp.pad(tail, ((0, LANES - rest), (0, 0))).T[:size, :rest]
        here = slice(i * LANES, i * LANES + size)
        out[here, LANES:] = (turn + term[here, LANES:]) * scale[:, LANES:]


def exchanged(tiles, axes):
    pieces = lax.axis_size(axes)
    got = lax.all_to_all(tiles.reshape(pieces, -1), axes, split_axis=0, concat_axis=0, tiled=True)
    return got.reshape(tiles.shape)


def step(snapshots, final_snapshot, pod_modes, right_vectors, inverse_sing, eigen_vectors):
    blocks = lax.axis_size("tm")
    rows, rank = snapshots.shape[0], right_vectors.shape[1]
    half = rows // (2 * blocks)
    me = lax.axis_index("tm").astype(jnp.int32)[None]
    sing = inverse_sing[None, :]

    def sent(value, distance):
        return lax.ppermute(value, "tm", [(i, (i + distance) % blocks) for i in range(blocks)])

    near, far = lax.axis_size(NEAR), lax.axis_size(FAR)
    lines = rank + 2 * (rank - LANES + BLOCKS)
    size = lines // near
    packed, snaps_in, final_in, vectors_in = call(
        term_kernel,
        (
            f32(lines, LANES),
            pltpu.VMEM(snapshots.shape, jnp.float32),
            pltpu.VMEM((1, rows), jnp.float32),
            pltpu.VMEM((rank, snapshots.shape[1]), jnp.float32),
        ),
        me,
        snapshots,
        final_snapshot[None, :],
        pod_modes.T,
        right_vectors.T,
        smem=1,
        hbm=(1, 2, 3, 4),
        scratch=(
            pltpu.VMEM((rank, rows), jnp.float32),
            pltpu.SemaphoreType.DMA((2 * (rows // CHUNK) + 2,)),
        ),
    )
    tiles = exchanged(packed, NEAR)

    to_right, to_left, right_later, left_later, own = call(
        shares_kernel,
        tuple(f32(rank + EXTRA, n * half) for n in (2, 2, 1, 1, 2)),
        me,
        snaps_in,
        final_in,
        vectors_in,
        smem=1,
    )
    from_left = sent(to_right, 1)
    from_right = sent(to_left, -1)

    copied = functools.partial(sum_and_copy_kernel, size=size)
    tiles = call(functools.partial(copied, copies=far), f32(far * size, LANES), tiles)
    tiles = exchanged(tiles, FAR)
    added = f32(rank + EXTRA, half)
    top = sent(call(functools.partial(add_kernel, side=0), added, right_later, from_left), 1)
    bottom = sent(call(functools.partial(add_kernel, side=1), added, left_later, from_right), -1)

    tiles = call(functools.partial(copied, copies=near), f32(near * size, LANES), tiles)
    tiles = exchanged(tiles, NEAR)
    dmd_modes, last_rows = call(
        dmd_kernel,
        (f32(rank, 2 * half), f32(BLOCKS, rank)),
        own,
        from_right,
        from_left,
        top,
        bottom,
        sing,
        eigen_vectors,
    )
    reduced_operator = call(operator_kernel, f32(rank, rank), tiles, last_rows, sing)
    return reduced_operator, dmd_modes.T


def solution(mesh):
    finer = Mesh(mesh.devices.reshape(4, 2, 4, 2, 2, mesh.shape["tm"]), (*SPACE, "tm"))
    return jax.shard_map(
        step,
        mesh=finer,
        in_specs=(P(SPACE, "tm"), P(SPACE), P(SPACE, None), P("tm", None), P(), P()),
        out_specs=(P(), P((*SPACE, "tm"), None)),
        check_vma=False,
    )
```

time: 84.6 us -> 73.4 us (0.87)
  waiting for transfers between devices: 12.5 us -> 7.32 us
  starting transfers between devices: 34.8 us -> 31.6 us
  blocking collectives: 24.8 us -> 23.3 us
  Pallas kernels: 8.71 us -> 9.97 us
  matrix products: 1.25 us -> 0 us
  local copies, waits for them, and re-layouts: 1.13 us -> 0.01 us
    all_to_all x2, waiting for transfers between devices: 9.05 us -> 0.01 us  [exchanged(): lax.all_to_all(tiles.reshape(pieces, -1), axes, split_axis=0, concat_axis...]
    ppermute x5 -> x4, starting transfers between devices: 18.8 us -> 12.8 us  [sent(): lax.ppermute(value, 'tm', [(i, (i + distance) % blocks) for i in range(bl...]
    ppermute x5 -> x4, waiting for transfers between devices: 3.41 us -> 7.32 us  [sent(): lax.ppermute(value, 'tm', [(i, (i + distance) % blocks) for i in range(bl...]
    all_to_all x2, starting transfers between devices: 16.1 us -> 18.8 us  [exchanged(): lax.all_to_all(tiles.reshape(pieces, -1), axes, split_axis=0, concat_axis...]
    all_to_all x1, blocking collectives: 24.8 us -> 23.3 us  [exchanged(): lax.all_to_all(tiles.reshape(pieces, -1), axes, split_axis=0, concat_axis...]
    pallas_call x6 -> x8, Pallas kernels: 8.71 us -> 9.97 us  [call(): pl.pallas_call(kernel, out_shape=outs, in_specs=specs, scratch_shapes=scr...]
    dot_general x1 -> x0, matrix products: 1.25 us -> none  [step(): lax.dot_general(eigen_vectors, scaled, (((0,), (0,)), ((), ())), precisio...]
    slice x1 -> x0, local copies, waits for them, and re-layouts: 1.11 us -> none  [step(): before = sent(right_vectors[-1], 1)]
  transfers between devices with their start and end apart: 7 -> 6, of which waited for: 3 -> 2; matrix products, arithmetic and copies ran while one was open for 2% -> 0% of each run, Pallas kernels for 9% -> 6%
where the time goes in v1:
time: 73.4 us; the launch traced here: 73 us
  starting transfers between devices  31.6 us (43%)
  blocking collectives  23.3 us (32%)
  Pallas kernels  9.97 us (14%)
  waiting for transfers between devices  7.32 us (10%)
  between operations  0.76 us (1%)
    all_to_all x1, blocking collectives, exchanged(): lax.all_to_all(tiles.reshape(pieces, -1), axes, split_axis=0, concat_axis...  23.3 us
    all_to_all x2, starting transfers between devices, exchanged(): lax.all_to_all(tiles.reshape(pieces, -1), axes, split_axis=0, concat_axis...  18.8 us
    ppermute x4, starting transfers between devices, sent(): lax.ppermute(value, 'tm', [(i, (i + distance) % blocks) for i in range(bl...  12.8 us
    pallas_call x8, Pallas kernels, call(): pl.pallas_call(kernel, out_shape=outs, in_specs=specs, scratch_shapes=scr...  9.97 us
    ppermute x4, waiting for transfers between devices, sent(): lax.ppermute(value, 'tm', [(i, (i + distance) % blocks) for i in range(bl...  7.32 us
  transfers between devices with their start and end apart: 6, of which 2 were waited for; matrix products, arithmetic and copies ran while one was open for 0% of the time, Pallas kernels for 6%

profile of v1, /device:TPU:1, one launch (start us, length us, event | category | flops | bytes accessed | tf_op | source)
XLA Modules:
  0.0 73.0 jit_solution(17273650674672271380)
XLA Ops:
  0.6 4.6 %shard_map.77 = (f32[352,128]{1,0:T(8,128)}, f32[2048,256]{1,0:T(8,128)S(1)}, f32[1,2048]{1,0:T(1,128)S(1)}, f32[200,256]{1,0:T(8,128)S(1)}) custom-call(s32[1]{0:T(128)} %bitcast.me, f32[2048,256]{1,0:T(8,128)} %snaps.1, f32[1,2048]{1,0:T(1,128)} %bitcast.20, f32[200,2048]{1,0:T(8,128)} %bitcast.18, f32[200,256]{1,0:T(8,128)} %bitcast.19), custom_call_target="tpu_custom_call" | custom-call | tf_op jit(solution)/shard_map/pallas_call | solution.py:34
  5.3 10.4 %all-to-all-start = ((f32[32,1,1408]{2,1,0:T(1,128)}), f32[32,1,1408]{2,1,0:T(1,128)S(1)}, u32[]{:S(2)}, u32[]{:S(2)}) async-start(f32[32,1,1408]{2,1,0:T(1,128)} %bitcast.4), calls=%async_computation | async-start | bytes 360448 | tf_op jit(solution)/shard_map/all_to_all | solution.py:206
  15.7 0.0 copy-start
  15.7 0.0 copy-start.1
  15.7 1.9 %shard_map.80 = (f32[208,512]{1,0:T(8,128)}, f32[208,512]{1,0:T(8,128)}, f32[208,256]{1,0:T(8,128)S(1)}, f32[208,256]{1,0:T(8,128)S(1)}, f32[208,512]{1,0:T(8,128)S(1)}) custom-call(s32[1]{0:T(128)} %bitcast.me, f32[2048,256]{1,0:T(8,128)S(1)} %get-tuple-element.14.snaps, f32[1,2048]{1,0:T(1,128)S(1)} %get-tuple-element.15.final, ...), custom_call_target="tpu_custom_call" | custom-call | tf_op jit(solution)/shard_map/pallas_call | solution.py:34
  17.6 4.5 %collective-permute-start = (f32[208,512]{1,0:T(8,128)}, f32[208,512]{1,0:T(8,128)S(1)}, u32[]{:S(2)}, u32[]{:S(2)}) collective-permute-start(f32[208,512]{1,0:T(8,128)} %get-tuple-element.18), channel_id=1, source_target_pairs={{0,3},{1,0},{2,1},{3,2},{4,7},{5,4},{6,5},{7,6},{8,11},{9,8},{10,9... | collective-permute-start | bytes 1277960 | tf_op jit(solution)/shard_map/ppermute | solution.py:218
  22.1 1.9 %collective-permute-start.1 = (f32[208,512]{1,0:T(8,128)}, f32[208,512]{1,0:T(8,128)S(1)}, u32[]{:S(2)}, u32[]{:S(2)}) collective-permute-start(f32[208,512]{1,0:T(8,128)} %get-tuple-element.19), channel_id=1, source_target_pairs={{0,1},{1,2},{2,3},{3,0},{4,5},{5,6},{6,7},{7,4},{8,9},{9,10},{10,1... | collective-permute-start | bytes 1277960 | tf_op jit(solution)/shard_map/ppermute | solution.py:218
  24.0 0.0 all-to-all-done
  24.0 23.3 %all_to_all.27 = f32[16,1,1408]{2,1,0:T(1,128)S(1)} all-to-all(f32[16,1,1408]{2,1,0:T(1,128)S(1)} %bitcast.14), channel_id=1, replica_groups=mesh['y_far'=4,'y_near'=2,'z_far'=4,'z_near'=2,'core'=2,'tm'=4] {'y_far'..., dimensions={0} | all-to-all | bytes 180224 | tf_op jit(solution)/shard_map/all_to_all | solution.py:206
  47.3 0.7 shard_map.79
  48.0 8.5 %all-to-all-start.2 = ((f32[32,1,1408]{2,1,0:T(1,128)}), f32[32,1,1408]{2,1,0:T(1,128)S(1)}, u32[]{:S(2)}, u32[]{:S(2)}) async-start(f32[32,1,1408]{2,1,0:T(1,128)} %bitcast.8), calls=%async_computation.2 | async-start | bytes 360448 | tf_op jit(solution)/shard_map/all_to_all | solution.py:206
  56.5 0.0 collective-permute-done.arrived.from_right
  56.5 4.5 %collective-permute-start.3 = (f32[208,256]{1,0:T(8,128)S(1)}, f32[208,256]{1,0:T(8,128)S(1)}, u32[]{:S(2)}, u32[]{:S(2)}) collective-permute-start(f32[208,256]{1,0:T(8,128)S(1)} %shard_map.82), channel_id=1, source_target_pairs={{0,3},{1,0},{2,1},{3,2},{4,7},{5,4},{6,5},{7,6},{8,11},{9,8},{10,9... | collective-permute-start | bytes 638984 | tf_op jit(solution)/shard_map/ppermute | solution.py:218
  61.0 0.0 collective-permute-done.1.arrived.from_left
  61.1 1.9 %collective-permute-start.2 = (f32[208,256]{1,0:T(8,128)S(1)}, f32[208,256]{1,0:T(8,128)S(1)}, u32[]{:S(2)}, u32[]{:S(2)}) collective-permute-start(f32[208,256]{1,0:T(8,128)S(1)} %shard_map.81), channel_id=1, source_target_pairs={{0,1},{1,2},{2,3},{3,0},{4,5},{5,6},{6,7},{7,4},{8,9},{9,10},{10,1... | collective-permute-start | bytes 638984 | tf_op jit(solution)/shard_map/ppermute | solution.py:218
  63.0 3.1 %collective-permute-done.3.bottom = f32[208,256]{1,0:T(8,128)S(1)} collective-permute-done((f32[208,256]{1,0:T(8,128)S(1)}, f32[208,256]{1,0:T(8,128)S(1)}, u32[]{:S(2)}, u32[]{:S(2)}) %collective-permute-start.3) | collective-permute-done | bytes 213024 | tf_op jit(solution)/shard_map/ppermute | solution.py:218
  66.1 4.2 %collective-permute-done.2.top = f32[208,256]{1,0:T(8,128)S(1)} collective-permute-done((f32[208,256]{1,0:T(8,128)S(1)}, f32[208,256]{1,0:T(8,128)S(1)}, u32[]{:S(2)}, u32[]{:S(2)}) %collective-permute-start.2) | collective-permute-done | bytes 213024 | tf_op jit(solution)/shard_map/ppermute | solution.py:218
  70.3 0.0 copy-done
  70.3 0.0 copy-done.1
  70.3 1.7 %shard_map.83 = (f32[200,512]{1,0:T(8,128)}, f32[4,200]{1,0:T(4,128)S(1)}) custom-call(f32[208,512]{1,0:T(8,128)S(1)} %get-tuple-element.17.own, f32[208,512]{1,0:T(8,128)S(1)} %collective-permute-done.arrived.from_right, f32[208,512]{1,0:T(8,128)S(1)} %collective-permute-done.1.arrived.from_left, f32[208,256]{1,0:T(8,128)S(1)} %collective-permute-done.2.top, ...), custom_call_target="tpu_custom_call" | custom-call | tf_op jit(solution)/shard_map/pallas_call | solution.py:34
  72.0 0.0 all-to-all-done.2
  72.0 1.0 %shard_map.84 = f32[200,200]{1,0:T(8,128)} custom-call(f32[352,128]{1,0:T(8,128)S(1)} %bitcast.12, f32[4,200]{1,0:T(4,128)S(1)} %get-tuple-element.22.rows, f32[1,200]{1,0:T(1,128)S(1)} %bitcast.17), custom_call_target="tpu_custom_call" | custom-call | tf_op jit(solution)/shard_map/pallas_call | solution.py:34
  (3 shorter events, 0.1 us)
Async XLA Ops:
  5.3 18.7 %all-to-all-start = ((f32[32,1,1408]{2,1,0:T(1,128)}), f32[32,1,1408]{2,1,0:T(1,128)S(1)}, u32[]{:S(2)}, u32[]{:S(2)}) async-start(f32[32,1,1408]{2,1,0:T(1,128)} %bitcast.4), calls=%async_computation | async-start | bytes 360448 | tf_op jit(solution)/shard_map/all_to_all | solution.py:206
  15.7 54.6 %copy-start = (f32[200,200]{1,0:T(8,128)S(1)}, f32[200,200]{1,0:T(8,128)}, u32[]{:S(2)}) copy-start(f32[200,200]{1,0:T(8,128)} %vectors.1) | copy-start | bytes 480004
  15.7 54.6 %copy-start.1 = (f32[200]{0:T(256)S(1)}, f32[200]{0:T(256)}, u32[]{:S(2)}) copy-start(f32[200]{0:T(256)} %param.10) | copy-start | bytes 2404
  17.6 38.9 %collective-permute-start = (f32[208,512]{1,0:T(8,128)}, f32[208,512]{1,0:T(8,128)S(1)}, u32[]{:S(2)}, u32[]{:S(2)}) collective-permute-start(f32[208,512]{1,0:T(8,128)} %get-tuple-element.18), channel_id=1, source_target_pairs={{0,3},{1,0},{2,1},{3,2},{4,7},{5,4},{6,5},{7,6},{8,11},{9,8},{10,9... | collective-permute-start | bytes 1277960 | tf_op jit(solution)/shard_map/ppermute | solution.py:218
  22.1 39.0 %collective-permute-start.1 = (f32[208,512]{1,0:T(8,128)}, f32[208,512]{1,0:T(8,128)S(1)}, u32[]{:S(2)}, u32[]{:S(2)}) collective-permute-start(f32[208,512]{1,0:T(8,128)} %get-tuple-element.19), channel_id=1, source_target_pairs={{0,1},{1,2},{2,3},{3,0},{4,5},{5,6},{6,7},{7,4},{8,9},{9,10},{10,1... | collective-permute-start | bytes 1277960 | tf_op jit(solution)/shard_map/ppermute | solution.py:218
  48.0 24.0 %all-to-all-start.2 = ((f32[32,1,1408]{2,1,0:T(1,128)}), f32[32,1,1408]{2,1,0:T(1,128)S(1)}, u32[]{:S(2)}, u32[]{:S(2)}) async-start(f32[32,1,1408]{2,1,0:T(1,128)} %bitcast.8), calls=%async_computation.2 | async-start | bytes 360448 | tf_op jit(solution)/shard_map/all_to_all | solution.py:206
  56.5 9.5 %collective-permute-start.3 = (f32[208,256]{1,0:T(8,128)S(1)}, f32[208,256]{1,0:T(8,128)S(1)}, u32[]{:S(2)}, u32[]{:S(2)}) collective-permute-start(f32[208,256]{1,0:T(8,128)S(1)} %shard_map.82), channel_id=1, source_target_pairs={{0,3},{1,0},{2,1},{3,2},{4,7},{5,4},{6,5},{7,6},{8,11},{9,8},{10,9... | collective-permute-start | bytes 638984 | tf_op jit(solution)/shard_map/ppermute | solution.py:218
  61.1 9.2 %collective-permute-start.2 = (f32[208,256]{1,0:T(8,128)S(1)}, f32[208,256]{1,0:T(8,128)S(1)}, u32[]{:S(2)}, u32[]{:S(2)}) collective-permute-start(f32[208,256]{1,0:T(8,128)S(1)} %shard_map.81), channel_id=1, source_target_pairs={{0,1},{1,2},{2,3},{3,0},{4,5},{5,6},{6,7},{7,4},{8,9},{9,10},{10,1... | collective-permute-start | bytes 638984 | tf_op jit(solution)/shard_map/ppermute | solution.py:218

commit v2 on v1

--- a/solution.py
+++ b/solution.py
@@ -118,42 +118,32 @@
         packed[rank + i * used : rank + (i + 1) * used, :] = turn[:used]
 
 
-def shares_kernel(
-    me, snaps, final, vectors, to_right, to_left, right_later, left_later, own
-):
+def shares_of(me, snaps, final, vectors):
     rank, snapshots = vectors.shape
-    half = right_later.shape[1]
+    points = snaps.shape[0]
     row = lax.broadcasted_iota(jnp.int32, (EXTRA, snapshots), 0)
     column = lax.broadcasted_iota(jnp.int32, (EXTRA, snapshots), 1)
-    unit = jnp.where((row == me[0]) & (column == 0), 1.0, 0.0)
-    left = split(jnp.concatenate([shifted(vectors[...]), unit], axis=0))
+    unit = jnp.where((row == me) & (column == 0), 1.0, 0.0)
+    left = split(jnp.concatenate([shifted(vectors), unit], axis=0))
     tail = jnp.pad(vectors[:, snapshots - LANES :], ((0, 2 * LANES - rank), (0, 0)))
-    last = jnp.concatenate([tail[:LANES].T[LANES - 1 :], tail[LANES:].T[LANES - 1 :]], axis=1)
-    slot = lax.broadcasted_iota(jnp.int32, (EXTRA, half), 0)
-    after = BLOCKS + lax.rem(me[0] + 1, BLOCKS)
-
-    def write(out, at, distance, side):
-        owner = lax.rem(me[0] + distance, BLOCKS)
-        here = pl.ds(pl.multiple_of(owner * (2 * half) + side * half, half), half)
-        block = three_pass(left, split(snaps[here, :]))
-        extra = jnp.where((slot == me[0]) & (me[0] == 0), final[:, here], block[rank:])
-        there = slice(at * half, (at + 1) * half)
-        out[:rank, there] = block[:rank]
-        out[rank:, there] = jnp.where(slot == after, last, extra)
-
-    write(to_right, 0, 2, 0)
-    write(to_right, 1, 1, 1)
-    write(to_left, 0, 3, 0)
-    write(to_left, 1, 2, 1)
-    write(right_later, 0, 1, 0)
-    write(left_later, 0, 3, 1)
-    write(own, 0, 0, 0)
-    write(own, 1, 0, 1)
-
-
-def add_kernel(later, arrived, out, *, side):
-    half = out.shape[1]
-    out[...] = later[...] + arrived[:, side * half : (side + 1) * half]
+    last = [tail[:LANES].T[LANES - 1 :], tail[LANES:].T[LANES - 1 :]]
+    last = jnp.concatenate(last * (points // (2 * LANES)), axis=1)
+    block = three_pass(left, split(snaps))
+    slot = lax.broadcasted_iota(jnp.int32, (EXTRA, points), 0)
+    extra = jnp.where((slot == me) & (me == 0), final, block[rank:])
+    extra = jnp.where(slot == BLOCKS + lax.rem(me + 1, BLOCKS), last, extra)
+    return block[:rank], extra
+
+
+def share_kernel(me, snaps, final, vectors, out, *, distance):
+    rank, points = vectors.shape[0], out.shape[1]
+    owner = lax.rem(me[0] + distance, BLOCKS)
+    here = pl.ds(pl.multiple_of(owner * points, points), points)
+    out[:rank, :], out[rank:, :] = shares_of(me[0], snaps[here, :], final[:, here], vectors[...])
+
+
+def add_kernel(own, arrived, out):
+    out[...] = own[...] + arrived[...]
 
 
 def sum_and_copy_kernel(tiles, out, *, size, copies):
@@ -164,20 +154,29 @@
         out[i * size : (i + 1) * size, :] = total
 
 
-def dmd_kernel(own, from_right, from_left, top, bottom, sing, vectors, out, rows):
-    rank = out.shape[0]
-    half = top.shape[1]
+def dmd_kernel(
+    me, snaps, final, vectors, from_right, from_left, sing, eigen, out, rows, snaps_in, final_in, vectors_in, sems
+):
+    rank, points = out.shape
+    here = pl.ds(pl.multiple_of(me[0] * points, points), points)
+    copies = (
+        pltpu.make_async_copy(vectors, vectors_in, sems.at[0]),
+        pltpu.make_async_copy(snaps.at[here, :], snaps_in, sems.at[1]),
+        pltpu.make_async_copy(final.at[:, here], final_in, sems.at[2]),
+    )
+    for copy in copies:
+        copy.start()
     scale = turned(sing[...])[:rank]
-    right = split(vectors[...])
-    for i, arrived in ((0, from_right[:, :half] + top[...]), (1, from_left[:, half:] + bottom[...])):
-        there = slice(i * half, (i + 1) * half)
-        total = own[:, there] + arrived
-        first = total[rank : rank + BLOCKS]
-        last = total[rank + BLOCKS :, :rank]
-        if i == 0:
-            rows[...] = last
-        summed = total[:rank] + three_pass(split(last), split(first), (0, 0))
-        out[:, there] = three_pass(right, split(summed * scale), (0, 0))
+    right = split(eigen[...])
+    arrived = from_right[...] + from_left[...]
+    for copy in copies:
+        copy.wait()
+    block, extra = shares_of(me[0], snaps_in[...], final_in[...], vectors_in[...])
+    extra = extra + arrived[rank:]
+    last = extra[BLOCKS:, :rank]
+    rows[...] = last
+    summed = block + arrived[:rank] + three_pass(split(last), split(extra[:BLOCKS]), (0, 0))
+    out[...] = three_pass(right, split(summed * scale), (0, 0))
 
 
 def operator_kernel(packed, rows, sing, out):
@@ -242,37 +241,42 @@
     )
     tiles = exchanged(packed, NEAR)
 
-    to_right, to_left, right_later, left_later, own = call(
-        shares_kernel,
-        tuple(f32(rank + EXTRA, n * half) for n in (2, 2, 1, 1, 2)),
-        me,
-        snaps_in,
-        final_in,
-        vectors_in,
-        smem=1,
-    )
-    from_left = sent(to_right, 1)
-    from_right = sent(to_left, -1)
+    share = f32(rank + EXTRA, 2 * half)
+
+    def share_for(distance):
+        kernel = functools.partial(share_kernel, distance=distance)
+        return call(kernel, share, me, snaps_in, final_in, vectors_in, smem=1)
+
+    two_right, left, one_right = share_for(2), share_for(3), share_for(1)
+    from_left = sent(two_right, 1)
 
     copied = functools.partial(sum_and_copy_kernel, size=size)
     tiles = call(functools.partial(copied, copies=far), f32(far * size, LANES), tiles)
     tiles = exchanged(tiles, FAR)
-    added = f32(rank + EXTRA, half)
-    top = sent(call(functools.partial(add_kernel, side=0), added, right_later, from_left), 1)
-    bottom = sent(call(functools.partial(add_kernel, side=1), added, left_later, from_right), -1)
+    from_left = sent(call(add_kernel, share, one_right, from_left), 1)
+    from_right = sent(left, -1)
 
     tiles = call(functools.partial(copied, copies=near), f32(near * size, LANES), tiles)
     tiles = exchanged(tiles, NEAR)
     dmd_modes, last_rows = call(
         dmd_kernel,
         (f32(rank, 2 * half), f32(BLOCKS, rank)),
-        own,
+        me,
+        snapshots,
+        final_snapshot[None, :],
+        right_vectors.T,
         from_right,
         from_left,
-        top,
-        bottom,
         sing,
         eigen_vectors,
+        smem=1,
+        hbm=(1, 2, 3),
+        scratch=(
+            pltpu.VMEM((2 * half, snapshots.shape[1]), jnp.float32),
+            pltpu.VMEM((1, 2 * half), jnp.float32),
+            pltpu.VMEM((rank, snapshots.shape[1]), jnp.float32),
+            pltpu.SemaphoreType.DMA((3,)),
+        ),
     )
     reduced_operator = call(operator_kernel, f32(rank, rank), tiles, last_rows, sing)
     return reduced_operator, dmd_modes.T

time: 73.4 us -> 62.3 us (0.85)
  blocking collectives: 23.3 us -> 0 us
  starting transfers between devices: 31.6 us -> 36.4 us
  waiting for transfers between devices: 7.32 us -> 11.8 us
  Pallas kernels: 9.97 us -> 12.9 us
    all_to_all x1 -> x0, blocking collectives: 23.3 us -> none  [exchanged(): lax.all_to_all(tiles.reshape(pieces, -1), axes, split_axis=0, concat_axis...]
    all_to_all x2 -> x3, waiting for transfers between devices: 0.01 us -> 11.8 us  [exchanged(): lax.all_to_all(tiles.reshape(pieces, -1), axes, split_axis=0, concat_axis...]
    all_to_all x2 -> x3, starting transfers between devices: 18.8 us -> 27.8 us  [exchanged(): lax.all_to_all(tiles.reshape(pieces, -1), axes, split_axis=0, concat_axis...]
    ppermute x4 -> x3, waiting for transfers between devices: 7.32 us -> 0.01 us  [sent(): lax.ppermute(value, 'tm', [(i, (i + distance) % blocks) for i in range(bl...]
    ppermute x4 -> x3, starting transfers between devices: 12.8 us -> 8.65 us  [sent(): lax.ppermute(value, 'tm', [(i, (i + distance) % blocks) for i in range(bl...]
    pallas_call x8 -> x9, Pallas kernels: 9.97 us -> 12.9 us  [call(): pl.pallas_call(kernel, out_shape=outs, in_specs=specs, scratch_shapes=scr...]
  transfers between devices with their start and end apart: 6 -> 6, of which waited for: 2 -> 3; matrix products, arithmetic and copies ran while one was open for 0% -> 0% of each run, Pallas kernels for 6% -> 12%
where the time goes in v2:
time: 62.3 us; the launch traced here: 61.8 us
  starting transfers between devices  36.4 us (58%)
  Pallas kernels  12.9 us (21%)
  waiting for transfers between devices  11.8 us (19%)
  between operations  0.75 us (1%)
    all_to_all x3, starting transfers between devices, exchanged(): lax.all_to_all(tiles.reshape(pieces, -1), axes, split_axis=0, concat_axis...  27.8 us
    pallas_call x9, Pallas kernels, call(): pl.pallas_call(kernel, out_shape=outs, in_specs=specs, scratch_shapes=scr...  12.9 us
    all_to_all x3, waiting for transfers between devices, exchanged(): lax.all_to_all(tiles.reshape(pieces, -1), axes, split_axis=0, concat_axis...  11.8 us
    ppermute x3, starting transfers between devices, sent(): lax.ppermute(value, 'tm', [(i, (i + distance) % blocks) for i in range(bl...  8.65 us
  transfers between devices with their start and end apart: 6, of which 3 were waited for; matrix products, arithmetic and copies ran while one was open for 0% of the time, Pallas kernels for 12%

profile of v2, /device:TPU:1, one launch (start us, length us, event | category | flops | bytes accessed | tf_op | source)
XLA Modules:
  0.0 61.8 jit_solution(15498893018523563609)
XLA Ops:
  0.6 4.6 %shard_map.77 = (f32[352,128]{1,0:T(8,128)}, f32[2048,256]{1,0:T(8,128)S(1)}, f32[1,2048]{1,0:T(1,128)S(1)}, f32[200,256]{1,0:T(8,128)S(1)}) custom-call(s32[1]{0:T(128)} %bitcast.me, f32[2048,256]{1,0:T(8,128)} %snaps.3, f32[1,2048]{1,0:T(1,128)} %bitcast.20, f32[200,2048]{1,0:T(8,128)} %bitcast.17, f32[200,256]{1,0:T(8,128)} %bitcast.18), custom_call_target="tpu_custom_call" | custom-call | tf_op jit(solution)/shard_map/pallas_call | solution.py:34
  5.3 10.4 %all-to-all-start = ((f32[32,1,1408]{2,1,0:T(1,128)}), f32[32,1,1408]{2,1,0:T(1,128)S(1)}, u32[]{:S(2)}, u32[]{:S(2)}) async-start(f32[32,1,1408]{2,1,0:T(1,128)} %bitcast.4), calls=%async_computation | async-start | bytes 360448 | tf_op jit(solution)/shard_map/all_to_all | solution.py:205
  15.7 1.2 %shard_map.82 = f32[208,512]{1,0:T(8,128)} custom-call(s32[1]{0:T(128)} %bitcast.me, f32[2048,256]{1,0:T(8,128)S(1)} %get-tuple-element.9.snaps, f32[1,2048]{1,0:T(1,128)S(1)} %get-tuple-element.10.final, f32[200,256]{1,0:T(8,128)S(1)} %get-tuple-element.11.vectors), custom_call_target="tpu_custom_call" | custom-call | tf_op jit(solution)/shard_map/pallas_call | solution.py:34
  16.9 3.3 %collective-permute-start.1 = (f32[208,512]{1,0:T(8,128)}, f32[208,512]{1,0:T(8,128)S(1)}, u32[]{:S(2)}, u32[]{:S(2)}) collective-permute-start(f32[208,512]{1,0:T(8,128)} %shard_map.82), channel_id=1, source_target_pairs={{0,1},{1,2},{2,3},{3,0},{4,5},{5,6},{6,7},{7,4},{8,9},{9,10},{10,1... | collective-permute-start | bytes 1277960 | tf_op jit(solution)/shard_map/ppermute | solution.py:217
  20.1 3.0 %all-to-all-done = f32[32,1,1408]{2,1,0:T(1,128)S(1)} async-done(((f32[32,1,1408]{2,1,0:T(1,128)}), f32[32,1,1408]{2,1,0:T(1,128)S(1)}, u32[]{:S(2)}, u32[]{:S(2)}) %all-to-all-start) | async-done | bytes 180256 | tf_op jit(solution)/shard_map/all_to_all | solution.py:205
  23.2 0.7 %shard_map.78 = f32[176,128]{1,0:T(8,128)} custom-call(f32[352,128]{1,0:T(8,128)S(1)} %bitcast.13), custom_call_target="tpu_custom_call" | custom-call | tf_op jit(solution)/shard_map/pallas_call | solution.py:34
  23.9 11.9 %all-to-all-start.1 = ((f32[16,1,1408]{2,1,0:T(1,128)}), f32[16,1,1408]{2,1,0:T(1,128)S(1)}, u32[]{:S(2)}, u32[]{:S(2)}) async-start(f32[16,1,1408]{2,1,0:T(1,128)} %bitcast.6), calls=%async_computation.1 | async-start | bytes 180224 | tf_op jit(solution)/shard_map/all_to_all | solution.py:205
  35.8 1.2 %shard_map.80 = f32[208,512]{1,0:T(8,128)} custom-call(s32[1]{0:T(128)} %bitcast.me, f32[2048,256]{1,0:T(8,128)S(1)} %get-tuple-element.9.snaps, f32[1,2048]{1,0:T(1,128)S(1)} %get-tuple-element.10.final, f32[200,256]{1,0:T(8,128)S(1)} %get-tuple-element.11.vectors), custom_call_target="tpu_custom_call" | custom-call | tf_op jit(solution)/shard_map/pallas_call | solution.py:34
  37.0 0.0 copy-start
  37.0 0.0 copy-start.1
  37.0 2.7 %collective-permute-start = (f32[208,512]{1,0:T(8,128)}, f32[208,512]{1,0:T(8,128)S(1)}, u32[]{:S(2)}, u32[]{:S(2)}) collective-permute-start(f32[208,512]{1,0:T(8,128)} %shard_map.80), channel_id=1, source_target_pairs={{0,3},{1,0},{2,1},{3,2},{4,7},{5,4},{6,5},{7,6},{8,11},{9,8},{10,9... | collective-permute-start | bytes 1277960 | tf_op jit(solution)/shard_map/ppermute | solution.py:217
  39.7 0.4 shard_map.81.own
  40.1 0.0 collective-permute-done.1.arrived
  40.1 0.1 shard_map.83
  40.2 2.7 %collective-permute-start.2 = (f32[208,512]{1,0:T(8,128)S(1)}, f32[208,512]{1,0:T(8,128)S(1)}, u32[]{:S(2)}, u32[]{:S(2)}) collective-permute-start(f32[208,512]{1,0:T(8,128)S(1)} %shard_map.83), channel_id=1, source_target_pairs={{0,1},{1,2},{2,3},{3,0},{4,5},{5,6},{6,7},{7,4},{8,9},{9,10},{10,1... | collective-permute-start | bytes 1277960 | tf_op jit(solution)/shard_map/ppermute | solution.py:217
  42.9 4.3 %all-to-all-done.1 = f32[16,1,1408]{2,1,0:T(1,128)S(1)} async-done(((f32[16,1,1408]{2,1,0:T(1,128)}), f32[16,1,1408]{2,1,0:T(1,128)S(1)}, u32[]{:S(2)}, u32[]{:S(2)}) %all-to-all-start.1) | async-done | bytes 90144 | tf_op jit(solution)/shard_map/all_to_all | solution.py:205
  47.2 0.7 %shard_map.79 = f32[352,128]{1,0:T(8,128)} custom-call(f32[176,128]{1,0:T(8,128)S(1)} %bitcast.14), custom_call_target="tpu_custom_call" | custom-call | tf_op jit(solution)/shard_map/pallas_call | solution.py:34
  47.9 5.5 %all-to-all-start.2 = ((f32[32,1,1408]{2,1,0:T(1,128)}), f32[32,1,1408]{2,1,0:T(1,128)S(1)}, u32[]{:S(2)}, u32[]{:S(2)}) async-start(f32[32,1,1408]{2,1,0:T(1,128)} %bitcast.8), calls=%async_computation.2 | async-start | bytes 360448 | tf_op jit(solution)/shard_map/all_to_all | solution.py:205
  53.4 0.0 collective-permute-done.from_right
  53.4 0.0 collective-permute-done.2.from_left
  53.4 0.0 copy-done
  53.4 0.0 copy-done.1
  53.4 3.0 %shard_map.84 = (f32[200,512]{1,0:T(8,128)}, f32[4,200]{1,0:T(4,128)S(1)}) custom-call(s32[1]{0:T(128)} %bitcast.me, f32[2048,256]{1,0:T(8,128)} %snaps.3, f32[1,2048]{1,0:T(1,128)} %bitcast.21, f32[200,256]{1,0:T(8,128)} %bitcast.19, f32[208,512]{1,0:T(8,128)S(1)} %collective-permute-done.from_right, f32[208,512]{1,0:T(8,128)S(1)} %collective-permute-done.2.from_left, ...), custom_call_target="tpu_custom_call" | custom-call | tf_op jit(solution)/shard_map/pallas_call | solution.py:34
  56.5 4.4 %all-to-all-done.2 = f32[32,1,1408]{2,1,0:T(1,128)S(1)} async-done(((f32[32,1,1408]{2,1,0:T(1,128)}), f32[32,1,1408]{2,1,0:T(1,128)S(1)}, u32[]{:S(2)}, u32[]{:S(2)}) %all-to-all-start.2) | async-done | bytes 180256 | tf_op jit(solution)/shard_map/all_to_all | solution.py:205
  60.9 1.0 %shard_map.85 = f32[200,200]{1,0:T(8,128)} custom-call(f32[352,128]{1,0:T(8,128)S(1)} %bitcast.12, f32[4,200]{1,0:T(4,128)S(1)} %get-tuple-element.12.rows, f32[1,200]{1,0:T(1,128)S(1)} %bitcast.16), custom_call_target="tpu_custom_call" | custom-call | tf_op jit(solution)/shard_map/pallas_call | solution.py:34
Async XLA Ops:
  5.3 17.9 %all-to-all-start = ((f32[32,1,1408]{2,1,0:T(1,128)}), f32[32,1,1408]{2,1,0:T(1,128)S(1)}, u32[]{:S(2)}, u32[]{:S(2)}) async-start(f32[32,1,1408]{2,1,0:T(1,128)} %bitcast.4), calls=%async_computation | async-start | bytes 360448 | tf_op jit(solution)/shard_map/all_to_all | solution.py:205
  16.9 23.3 %collective-permute-start.1 = (f32[208,512]{1,0:T(8,128)}, f32[208,512]{1,0:T(8,128)S(1)}, u32[]{:S(2)}, u32[]{:S(2)}) collective-permute-start(f32[208,512]{1,0:T(8,128)} %shard_map.82), channel_id=1, source_target_pairs={{0,1},{1,2},{2,3},{3,0},{4,5},{5,6},{6,7},{7,4},{8,9},{9,10},{10,1... | collective-permute-start | bytes 1277960 | tf_op jit(solution)/shard_map/ppermute | solution.py:217
  23.9 23.3 %all-to-all-start.1 = ((f32[16,1,1408]{2,1,0:T(1,128)}), f32[16,1,1408]{2,1,0:T(1,128)S(1)}, u32[]{:S(2)}, u32[]{:S(2)}) async-start(f32[16,1,1408]{2,1,0:T(1,128)} %bitcast.6), calls=%async_computation.1 | async-start | bytes 180224 | tf_op jit(solution)/shard_map/all_to_all | solution.py:205
  37.0 16.4 %copy-start = (f32[200,200]{1,0:T(8,128)S(1)}, f32[200,200]{1,0:T(8,128)}, u32[]{:S(2)}) copy-start(f32[200,200]{1,0:T(8,128)} %eigen.1) | copy-start | bytes 480004
  37.0 16.5 %copy-start.1 = (f32[200]{0:T(256)S(1)}, f32[200]{0:T(256)}, u32[]{:S(2)}) copy-start(f32[200]{0:T(256)} %param.10) | copy-start | bytes 2404
  37.0 16.4 %collective-permute-start = (f32[208,512]{1,0:T(8,128)}, f32[208,512]{1,0:T(8,128)S(1)}, u32[]{:S(2)}, u32[]{:S(2)}) collective-permute-start(f32[208,512]{1,0:T(8,128)} %shard_map.80), channel_id=1, source_target_pairs={{0,3},{1,0},{2,1},{3,2},{4,7},{5,4},{6,5},{7,6},{8,11},{9,8},{10,9... | collective-permute-start | bytes 1277960 | tf_op jit(solution)/shard_map/ppermute | solution.py:217
  40.2 13.2 %collective-permute-start.2 = (f32[208,512]{1,0:T(8,128)S(1)}, f32[208,512]{1,0:T(8,128)S(1)}, u32[]{:S(2)}, u32[]{:S(2)}) collective-permute-start(f32[208,512]{1,0:T(8,128)S(1)} %shard_map.83), channel_id=1, source_target_pairs={{0,1},{1,2},{2,3},{3,0},{4,5},{5,6},{6,7},{7,4},{8,9},{9,10},{10,1... | collective-permute-start | bytes 1277960 | tf_op jit(solution)/shard_map/ppermute | solution.py:217
  47.9 13.0 %all-to-all-start.2 = ((f32[32,1,1408]{2,1,0:T(1,128)}), f32[32,1,1408]{2,1,0:T(1,128)S(1)}, u32[]{:S(2)}, u32[]{:S(2)}) async-start(f32[32,1,1408]{2,1,0:T(1,128)} %bitcast.8), calls=%async_computation.2 | async-start | bytes 360448 | tf_op jit(solution)/shard_map/all_to_all | solution.py:205

commit v3 on v2

--- a/solution.py
+++ b/solution.py
@@ -2,6 +2,7 @@
 
 import jax
 import jax.numpy as jnp
+import numpy as np
 from jax import lax
 from jax.experimental import pallas as pl
 from jax.experimental.pallas import tpu as pltpu
@@ -9,8 +10,11 @@
 from jax.sharding import PartitionSpec as P
 
 SPACE = ("y_far", "y_near", "z_far", "z_near", "core")
+ALL = (*SPACE, "tm")
 NEAR = ("y_near", "z_near", "core", "tm")
 FAR = ("y_far", "z_far")
+NEAR_FIRST = (1, 1, 1, 2)
+FAR_FIRST = (2, 3)
 LANES = 128
 BLOCKS = 4
 EXTRA = 2 * BLOCKS
@@ -200,9 +204,21 @@
         out[here, LANES:] = (turn + term[here, LANES:]) * scale[:, LANES:]
 
 
-def exchanged(tiles, axes):
-    pieces = lax.axis_size(axes)
-    got = lax.all_to_all(tiles.reshape(pieces, -1), axes, split_axis=0, concat_axis=0, tiled=True)
+def groups_of(axes, first):
+    sizes = {axis: lax.axis_size(axis) for axis in ALL}
+    places = np.arange(np.prod(list(sizes.values()))).reshape(*sizes.values())
+    for axis, start in zip(axes, first, strict=True):
+        places = np.roll(places, -start, ALL.index(axis))
+    others = [i for i, axis in enumerate(ALL) if axis not in axes]
+    places = places.transpose(*others, *(ALL.index(axis) for axis in axes))
+    return places.reshape(-1, int(np.prod([sizes[axis] for axis in axes]))).tolist()
+
+
+def exchanged(tiles, groups):
+    pieces = tiles.reshape(len(groups[0]), -1)
+    got = lax.all_to_all(
+        pieces, ALL, split_axis=0, concat_axis=0, tiled=True, axis_index_groups=groups
+    )
     return got.reshape(tiles.shape)
 
 
@@ -217,6 +233,7 @@
         return lax.ppermute(value, "tm", [(i, (i + distance) % blocks) for i in range(blocks)])
 
     near, far = lax.axis_size(NEAR), lax.axis_size(FAR)
+    near_groups, far_groups = groups_of(NEAR, NEAR_FIRST), groups_of(FAR, FAR_FIRST)
     lines = rank + 2 * (rank - LANES + BLOCKS)
     size = lines // near
     packed, snaps_in, final_in, vectors_in = call(
@@ -239,7 +256,7 @@
             pltpu.SemaphoreType.DMA((2 * (rows // CHUNK) + 2,)),
         ),
     )
-    tiles = exchanged(packed, NEAR)
+    tiles = exchanged(packed, near_groups)
 
     share = f32(rank + EXTRA, 2 * half)
 
@@ -252,12 +269,12 @@
 
     copied = functools.partial(sum_and_copy_kernel, size=size)
     tiles = call(functools.partial(copied, copies=far), f32(far * size, LANES), tiles)
-    tiles = exchanged(tiles, FAR)
+    tiles = exchanged(tiles, far_groups)
     from_left = sent(call(add_kernel, share, one_right, from_left), 1)
     from_right = sent(left, -1)
 
     tiles = call(functools.partial(copied, copies=near), f32(near * size, LANES), tiles)
-    tiles = exchanged(tiles, NEAR)
+    tiles = exchanged(tiles, near_groups)
     dmd_modes, last_rows = call(
         dmd_kernel,
         (f32(rank, 2 * half), f32(BLOCKS, rank)),

time: 62.3 us -> 60.4 us (0.970)
  waiting for transfers between devices: 11.8 us -> 3.79 us
  starting transfers between devices: 36.4 us -> 42.6 us
    all_to_all x3, waiting for transfers between devices: 11.8 us -> 0.22 us  [exchanged(): lax.all_to_all(pieces, ALL, split_axis=0, concat_axis=0, tiled=True, axis...]
    all_to_all x3, starting transfers between devices: 27.8 us -> 34.3 us  [exchanged(): lax.all_to_all(pieces, ALL, split_axis=0, concat_axis=0, tiled=True, axis...]
    ppermute x3, waiting for transfers between devices: 0.01 us -> 3.57 us  [sent(): lax.ppermute(value, 'tm', [(i, (i + distance) % blocks) for i in range(bl...]
  transfers between devices with their start and end apart: 6 -> 6, of which waited for: 3 -> 2; matrix products, arithmetic and copies ran while one was open for 0% -> 0% of each run, Pallas kernels for 12% -> 12%
where the time goes in v3:
time: 60.4 us; the launch traced here: 60 us
  starting transfers between devices  42.6 us (71%)
  Pallas kernels  12.9 us (21%)
  waiting for transfers between devices  3.79 us (6%)
  between operations  0.73 us (1%)
    all_to_all x3, starting transfers between devices, exchanged(): lax.all_to_all(pieces, ALL, split_axis=0, concat_axis=0, tiled=True, axis...  34.3 us
    pallas_call x9, Pallas kernels, call(): pl.pallas_call(kernel, out_shape=outs, in_specs=specs, scratch_shapes=scr...  12.9 us
    ppermute x3, starting transfers between devices, sent(): lax.ppermute(value, 'tm', [(i, (i + distance) % blocks) for i in range(bl...  8.32 us
    ppermute x3, waiting for transfers between devices, sent(): lax.ppermute(value, 'tm', [(i, (i + distance) % blocks) for i in range(bl...  3.57 us
  transfers between devices with their start and end apart: 6, of which 2 were waited for; matrix products, arithmetic and copies ran while one was open for 0% of the time, Pallas kernels for 12%

profile of v3, /device:TPU:1, one launch (start us, length us, event | category | flops | bytes accessed | tf_op | source)
XLA Modules:
  0.0 60.0 jit_solution(16209059747593014895)
XLA Ops:
  0.6 4.6 %shard_map.77 = (f32[352,128]{1,0:T(8,128)}, f32[2048,256]{1,0:T(8,128)S(1)}, f32[1,2048]{1,0:T(1,128)S(1)}, f32[200,256]{1,0:T(8,128)S(1)}) custom-call(s32[1]{0:T(128)} %bitcast.me, f32[2048,256]{1,0:T(8,128)} %snaps.3, f32[1,2048]{1,0:T(1,128)} %bitcast.20, f32[200,2048]{1,0:T(8,128)} %bitcast.17, f32[200,256]{1,0:T(8,128)} %bitcast.18), custom_call_target="tpu_custom_call" | custom-call | tf_op jit(solution)/shard_map/pallas_call | solution.py:38
  5.3 13.0 %all-to-all-start = ((f32[32,1,1408]{2,1,0:T(1,128)}), f32[32,1,1408]{2,1,0:T(1,128)S(1)}, u32[]{:S(2)}, u32[]{:S(2)}) async-start(f32[32,1,1408]{2,1,0:T(1,128)} %bitcast.4), calls=%async_computation | async-start | bytes 360448 | tf_op jit(solution)/shard_map/all_to_all | solution.py:219
  18.3 1.2 %shard_map.82 = f32[208,512]{1,0:T(8,128)} custom-call(s32[1]{0:T(128)} %bitcast.me, f32[2048,256]{1,0:T(8,128)S(1)} %get-tuple-element.9.snaps, f32[1,2048]{1,0:T(1,128)S(1)} %get-tuple-element.10.final, f32[200,256]{1,0:T(8,128)S(1)} %get-tuple-element.11.vectors), custom_call_target="tpu_custom_call" | custom-call | tf_op jit(solution)/shard_map/pallas_call | solution.py:38
  19.5 1.9 %collective-permute-start.1 = (f32[208,512]{1,0:T(8,128)}, f32[208,512]{1,0:T(8,128)S(1)}, u32[]{:S(2)}, u32[]{:S(2)}) collective-permute-start(f32[208,512]{1,0:T(8,128)} %shard_map.82), channel_id=1, source_target_pairs={{0,1},{1,2},{2,3},{3,0},{4,5},{5,6},{6,7},{7,4},{8,9},{9,10},{10,1... | collective-permute-start | bytes 1277960 | tf_op jit(solution)/shard_map/ppermute | solution.py:233
  21.4 0.2 all-to-all-done
  21.6 0.7 %shard_map.78 = f32[176,128]{1,0:T(8,128)} custom-call(f32[352,128]{1,0:T(8,128)S(1)} %bitcast.13), custom_call_target="tpu_custom_call" | custom-call | tf_op jit(solution)/shard_map/pallas_call | solution.py:38
  22.3 12.7 %all-to-all-start.1 = ((f32[16,1,1408]{2,1,0:T(1,128)}), f32[16,1,1408]{2,1,0:T(1,128)S(1)}, u32[]{:S(2)}, u32[]{:S(2)}) async-start(f32[16,1,1408]{2,1,0:T(1,128)} %bitcast.6), calls=%async_computation.1 | async-start | bytes 180224 | tf_op jit(solution)/shard_map/all_to_all | solution.py:219
  35.0 1.2 %shard_map.80 = f32[208,512]{1,0:T(8,128)} custom-call(s32[1]{0:T(128)} %bitcast.me, f32[2048,256]{1,0:T(8,128)S(1)} %get-tuple-element.9.snaps, f32[1,2048]{1,0:T(1,128)S(1)} %get-tuple-element.10.final, f32[200,256]{1,0:T(8,128)S(1)} %get-tuple-element.11.vectors), custom_call_target="tpu_custom_call" | custom-call | tf_op jit(solution)/shard_map/pallas_call | solution.py:38
  36.2 0.0 copy-start
  36.2 0.0 copy-start.1
  36.2 4.5 %collective-permute-start = (f32[208,512]{1,0:T(8,128)}, f32[208,512]{1,0:T(8,128)S(1)}, u32[]{:S(2)}, u32[]{:S(2)}) collective-permute-start(f32[208,512]{1,0:T(8,128)} %shard_map.80), channel_id=1, source_target_pairs={{0,3},{1,0},{2,1},{3,2},{4,7},{5,4},{6,5},{7,6},{8,11},{9,8},{10,9... | collective-permute-start | bytes 1277960 | tf_op jit(solution)/shard_map/ppermute | solution.py:233
  40.7 0.4 shard_map.81.own
  41.1 0.0 collective-permute-done.1.arrived
  41.1 0.1 shard_map.83
  41.2 1.9 %collective-permute-start.2 = (f32[208,512]{1,0:T(8,128)S(1)}, f32[208,512]{1,0:T(8,128)S(1)}, u32[]{:S(2)}, u32[]{:S(2)}) collective-permute-start(f32[208,512]{1,0:T(8,128)S(1)} %shard_map.83), channel_id=1, source_target_pairs={{0,1},{1,2},{2,3},{3,0},{4,5},{5,6},{6,7},{7,4},{8,9},{9,10},{10,1... | collective-permute-start | bytes 1277960 | tf_op jit(solution)/shard_map/ppermute | solution.py:233
  43.1 0.0 all-to-all-done.1
  43.1 0.7 %shard_map.79 = f32[352,128]{1,0:T(8,128)} custom-call(f32[176,128]{1,0:T(8,128)S(1)} %bitcast.14), custom_call_target="tpu_custom_call" | custom-call | tf_op jit(solution)/shard_map/pallas_call | solution.py:38
  43.8 8.6 %all-to-all-start.2 = ((f32[32,1,1408]{2,1,0:T(1,128)}), f32[32,1,1408]{2,1,0:T(1,128)S(1)}, u32[]{:S(2)}, u32[]{:S(2)}) async-start(f32[32,1,1408]{2,1,0:T(1,128)} %bitcast.8), calls=%async_computation.2 | async-start | bytes 360448 | tf_op jit(solution)/shard_map/all_to_all | solution.py:219
  52.4 0.0 collective-permute-done.from_right
  52.4 3.6 %collective-permute-done.2.from_left = f32[208,512]{1,0:T(8,128)S(1)} collective-permute-done((f32[208,512]{1,0:T(8,128)S(1)}, f32[208,512]{1,0:T(8,128)S(1)}, u32[]{:S(2)}, u32[]{:S(2)}) %collective-permute-start.2) | collective-permute-done | bytes 426016 | tf_op jit(solution)/shard_map/ppermute | solution.py:233
  56.0 0.0 copy-done
  56.0 0.0 copy-done.1
  56.0 3.0 %shard_map.84 = (f32[200,512]{1,0:T(8,128)}, f32[4,200]{1,0:T(4,128)S(1)}) custom-call(s32[1]{0:T(128)} %bitcast.me, f32[2048,256]{1,0:T(8,128)} %snaps.3, f32[1,2048]{1,0:T(1,128)} %bitcast.21, f32[200,256]{1,0:T(8,128)} %bitcast.19, f32[208,512]{1,0:T(8,128)S(1)} %collective-permute-done.from_right, f32[208,512]{1,0:T(8,128)S(1)} %collective-permute-done.2.from_left, ...), custom_call_target="tpu_custom_call" | custom-call | tf_op jit(solution)/shard_map/pallas_call | solution.py:38
  59.0 0.0 all-to-all-done.2
  59.0 1.0 %shard_map.85 = f32[200,200]{1,0:T(8,128)} custom-call(f32[352,128]{1,0:T(8,128)S(1)} %bitcast.12, f32[4,200]{1,0:T(4,128)S(1)} %get-tuple-element.12.rows, f32[1,200]{1,0:T(1,128)S(1)} %bitcast.16), custom_call_target="tpu_custom_call" | custom-call | tf_op jit(solution)/shard_map/pallas_call | solution.py:38
Async XLA Ops:
  5.3 16.3 %all-to-all-start = ((f32[32,1,1408]{2,1,0:T(1,128)}), f32[32,1,1408]{2,1,0:T(1,128)S(1)}, u32[]{:S(2)}, u32[]{:S(2)}) async-start(f32[32,1,1408]{2,1,0:T(1,128)} %bitcast.4), calls=%async_computation | async-start | bytes 360448 | tf_op jit(solution)/shard_map/all_to_all | solution.py:219
  19.5 21.7 %collective-permute-start.1 = (f32[208,512]{1,0:T(8,128)}, f32[208,512]{1,0:T(8,128)S(1)}, u32[]{:S(2)}, u32[]{:S(2)}) collective-permute-start(f32[208,512]{1,0:T(8,128)} %shard_map.82), channel_id=1, source_target_pairs={{0,1},{1,2},{2,3},{3,0},{4,5},{5,6},{6,7},{7,4},{8,9},{9,10},{10,1... | collective-permute-start | bytes 1277960 | tf_op jit(solution)/shard_map/ppermute | solution.py:233
  22.3 20.8 %all-to-all-start.1 = ((f32[16,1,1408]{2,1,0:T(1,128)}), f32[16,1,1408]{2,1,0:T(1,128)S(1)}, u32[]{:S(2)}, u32[]{:S(2)}) async-start(f32[16,1,1408]{2,1,0:T(1,128)} %bitcast.6), calls=%async_computation.1 | async-start | bytes 180224 | tf_op jit(solution)/shard_map/all_to_all | solution.py:219
  36.2 19.8 %copy-start = (f32[200,200]{1,0:T(8,128)S(1)}, f32[200,200]{1,0:T(8,128)}, u32[]{:S(2)}) copy-start(f32[200,200]{1,0:T(8,128)} %eigen.1) | copy-start | bytes 480004
  36.2 19.8 %copy-start.1 = (f32[200]{0:T(256)S(1)}, f32[200]{0:T(256)}, u32[]{:S(2)}) copy-start(f32[200]{0:T(256)} %param.10) | copy-start | bytes 2404
  36.2 16.2 %collective-permute-start = (f32[208,512]{1,0:T(8,128)}, f32[208,512]{1,0:T(8,128)S(1)}, u32[]{:S(2)}, u32[]{:S(2)}) collective-permute-start(f32[208,512]{1,0:T(8,128)} %shard_map.80), channel_id=1, source_target_pairs={{0,3},{1,0},{2,1},{3,2},{4,7},{5,4},{6,5},{7,6},{8,11},{9,8},{10,9... | collective-permute-start | bytes 1277960 | tf_op jit(solution)/shard_map/ppermute | solution.py:233
  41.2 14.8 %collective-permute-start.2 = (f32[208,512]{1,0:T(8,128)S(1)}, f32[208,512]{1,0:T(8,128)S(1)}, u32[]{:S(2)}, u32[]{:S(2)}) collective-permute-start(f32[208,512]{1,0:T(8,128)S(1)} %shard_map.83), channel_id=1, source_target_pairs={{0,1},{1,2},{2,3},{3,0},{4,5},{5,6},{6,7},{7,4},{8,9},{9,10},{10,1... | collective-permute-start | bytes 1277960 | tf_op jit(solution)/shard_map/ppermute | solution.py:233
  43.8 15.2 %all-to-all-start.2 = ((f32[32,1,1408]{2,1,0:T(1,128)}), f32[32,1,1408]{2,1,0:T(1,128)S(1)}, u32[]{:S(2)}, u32[]{:S(2)}) async-start(f32[32,1,1408]{2,1,0:T(1,128)} %bitcast.8), calls=%async_computation.2 | async-start | bytes 360448 | tf_op jit(solution)/shard_map/all_to_all | solution.py:219

commit v4 on v3

--- a/solution.py
+++ b/solution.py
@@ -90,26 +90,27 @@
     ]
     got_final = pltpu.make_async_copy(final, final_in, sems.at[2 * chunks])
     got_vectors = pltpu.make_async_copy(vectors, vectors_in, sems.at[2 * chunks + 1])
+    got_final.start()
     for i in range(chunks):
         got_modes[i].start()
         got_snaps[i].start()
-    got_final.start()
     got_vectors.start()
 
     total = of_final = None
+    got_final.wait()
     for i, here in enumerate(spans):
         got_modes[i].wait()
         got_snaps[i].wait()
-        left = split(modes_in[:, here])
-        product = three_pass(left, split(snaps_in[here, :]), (1, 0))
-        if i == 0:
-            got_final.wait()
-        column = three_pass(left, split(jnp.broadcast_to(final_in[:, here], (8, CHUNK))))
+        left, last = modes_in[:, here], final_in[:, here]
+        product = three_pass(split(left), split(snaps_in[here, :]), (1, 0))
         total = product if total is None else total + product
-        of_final = column if of_final is None else of_final + column
+        for j in range(0, CHUNK, LANES):
+            column = left[:, j : j + LANES] * last[:, j : j + LANES]
+            of_final = column if of_final is None else of_final + column
     got_vectors.wait()
     whole = three_pass(split(total), split(shifted(vectors_in[...])))
-    first = jnp.where(me[0] == 0, of_final[:, :1], total[:, :1])
+    of_final = jnp.sum(of_final, axis=1, keepdims=True)
+    first = jnp.where(me[0] == 0, of_final, total[:, :1])
     packed[:rank, :] = whole[:, :LANES]
     rest = rank - LANES
     tail = jnp.pad(whole[:, LANES:], ((0, 0), (0, LANES - rest)))
@@ -158,10 +159,8 @@
         out[i * size : (i + 1) * size, :] = total
 
 
-def dmd_kernel(
-    me, snaps, final, vectors, from_right, from_left, sing, eigen, out, rows, snaps_in, final_in, vectors_in, sems
-):
-    rank, points = out.shape
+def own_share_kernel(me, snaps, final, vectors, out, snaps_in, final_in, vectors_in, sems):
+    rank, points = vectors.shape[0], out.shape[1]
     here = pl.ds(pl.multiple_of(me[0] * points, points), points)
     copies = (
         pltpu.make_async_copy(vectors, vectors_in, sems.at[0]),
@@ -170,17 +169,20 @@
     )
     for copy in copies:
         copy.start()
-    scale = turned(sing[...])[:rank]
-    right = split(eigen[...])
-    arrived = from_right[...] + from_left[...]
     for copy in copies:
         copy.wait()
-    block, extra = shares_of(me[0], snaps_in[...], final_in[...], vectors_in[...])
-    extra = extra + arrived[rank:]
-    last = extra[BLOCKS:, :rank]
+    out[:rank, :], out[rank:, :] = shares_of(me[0], snaps_in[...], final_in[...], vectors_in[...])
+
+
+def dmd_kernel(own, from_right, from_left, sing, eigen, out, rows):
+    rank = out.shape[0]
+    scale = turned(sing[...])[:rank]
+    total = own[...] + from_right[...] + from_left[...]
+    first = total[rank : rank + BLOCKS]
+    last = total[rank + BLOCKS :, :rank]
     rows[...] = last
-    summed = block + arrived[:rank] + three_pass(split(last), split(extra[:BLOCKS]), (0, 0))
-    out[...] = three_pass(right, split(summed * scale), (0, 0))
+    summed = total[:rank] + three_pass(split(last), split(first), (0, 0))
+    out[...] = three_pass(split(eigen[...]), split(summed * scale), (0, 0))
 
 
 def operator_kernel(packed, rows, sing, out):
@@ -275,17 +277,13 @@
 
     tiles = call(functools.partial(copied, copies=near), f32(near * size, LANES), tiles)
     tiles = exchanged(tiles, near_groups)
-    dmd_modes, last_rows = call(
-        dmd_kernel,
-        (f32(rank, 2 * half), f32(BLOCKS, rank)),
+    own = call(
+        own_share_kernel,
+        share,
         me,
         snapshots,
         final_snapshot[None, :],
         right_vectors.T,
-        from_right,
-        from_left,
-        sing,
-        eigen_vectors,
         smem=1,
         hbm=(1, 2, 3),
         scratch=(
@@ -295,6 +293,15 @@
             pltpu.SemaphoreType.DMA((3,)),
         ),
     )
+    dmd_modes, last_rows = call(
+        dmd_kernel,
+        (f32(rank, 2 * half), f32(BLOCKS, rank)),
+        own,
+        from_right,
+        from_left,
+        sing,
+        eigen_vectors,
+    )
     reduced_operator = call(operator_kernel, f32(rank, rank), tiles, last_rows, sing)
     return reduced_operator, dmd_modes.T
 

time: 60.4 us -> 58.8 us (0.974)
  waiting for transfers between devices: 3.79 us -> 2.68 us
    ppermute x3, waiting for transfers between devices: 3.57 us -> 1.94 us  [sent(): lax.ppermute(value, 'tm', [(i, (i + distance) % blocks) for i in range(bl...]
    pallas_call x9 -> x10, Pallas kernels: 12.9 us -> 12.3 us  [call(): pl.pallas_call(kernel, out_shape=outs, in_specs=specs, scratch_shapes=scr...]
  transfers between devices with their start and end apart: 6 -> 6, of which waited for: 2 -> 3; matrix products, arithmetic and copies ran while one was open for 0% -> 0% of each run, Pallas kernels for 12% -> 13%
where the time goes in v4:
time: 58.8 us; the launch traced here: 58.3 us
  starting transfers between devices  42.6 us (72%)
  Pallas kernels  12.3 us (21%)
  waiting for transfers between devices  2.68 us (5%)
  between operations  0.74 us (1%)
    all_to_all x3, starting transfers between devices, exchanged(): lax.all_to_all(pieces, ALL, split_axis=0, concat_axis=0, tiled=True, axis...  34.3 us
    pallas_call x10, Pallas kernels, call(): pl.pallas_call(kernel, out_shape=outs, in_specs=specs, scratch_shapes=scr...  12.3 us
    ppermute x3, starting transfers between devices, sent(): lax.ppermute(value, 'tm', [(i, (i + distance) % blocks) for i in range(bl...  8.31 us
    ppermute x3, waiting for transfers between devices, sent(): lax.ppermute(value, 'tm', [(i, (i + distance) % blocks) for i in range(bl...  1.94 us
  transfers between devices with their start and end apart: 6, of which 3 were waited for; matrix products, arithmetic and copies ran while one was open for 0% of the time, Pallas kernels for 13%

profile of v4, /device:TPU:1, one launch (start us, length us, event | category | flops | bytes accessed | tf_op | source)
XLA Modules:
  0.0 58.3 jit_solution(12728509238371439854)
XLA Ops:
  0.6 4.0 %shard_map.77 = (f32[352,128]{1,0:T(8,128)}, f32[2048,256]{1,0:T(8,128)S(1)}, f32[1,2048]{1,0:T(1,128)S(1)}, f32[200,256]{1,0:T(8,128)S(1)}) custom-call(s32[1]{0:T(128)} %bitcast.me, f32[2048,256]{1,0:T(8,128)} %snaps.3, f32[1,2048]{1,0:T(1,128)} %bitcast.20, f32[200,2048]{1,0:T(8,128)} %bitcast.17, f32[200,256]{1,0:T(8,128)} %bitcast.18), custom_call_target="tpu_custom_call" | custom-call | tf_op jit(solution)/shard_map/pallas_call | solution.py:38
  4.7 13.0 %all-to-all-start = ((f32[32,1,1408]{2,1,0:T(1,128)}), f32[32,1,1408]{2,1,0:T(1,128)S(1)}, u32[]{:S(2)}, u32[]{:S(2)}) async-start(f32[32,1,1408]{2,1,0:T(1,128)} %bitcast.4), calls=%async_computation | async-start | bytes 360448 | tf_op jit(solution)/shard_map/all_to_all | solution.py:221
  17.7 1.2 %shard_map.83 = f32[208,512]{1,0:T(8,128)} custom-call(s32[1]{0:T(128)} %bitcast.me, f32[2048,256]{1,0:T(8,128)S(1)} %get-tuple-element.9.snaps, f32[1,2048]{1,0:T(1,128)S(1)} %get-tuple-element.10.final, f32[200,256]{1,0:T(8,128)S(1)} %get-tuple-element.11.vectors), custom_call_target="tpu_custom_call" | custom-call | tf_op jit(solution)/shard_map/pallas_call | solution.py:38
  18.9 1.9 %collective-permute-start.1 = (f32[208,512]{1,0:T(8,128)}, f32[208,512]{1,0:T(8,128)S(1)}, u32[]{:S(2)}, u32[]{:S(2)}) collective-permute-start(f32[208,512]{1,0:T(8,128)} %shard_map.83), channel_id=1, source_target_pairs={{0,1},{1,2},{2,3},{3,0},{4,5},{5,6},{6,7},{7,4},{8,9},{9,10},{10,1... | collective-permute-start | bytes 1277960 | tf_op jit(solution)/shard_map/ppermute | solution.py:235
  20.8 0.2 all-to-all-done
  21.0 0.7 %shard_map.78 = f32[176,128]{1,0:T(8,128)} custom-call(f32[352,128]{1,0:T(8,128)S(1)} %bitcast.13), custom_call_target="tpu_custom_call" | custom-call | tf_op jit(solution)/shard_map/pallas_call | solution.py:38
  21.7 12.7 %all-to-all-start.1 = ((f32[16,1,1408]{2,1,0:T(1,128)}), f32[16,1,1408]{2,1,0:T(1,128)S(1)}, u32[]{:S(2)}, u32[]{:S(2)}) async-start(f32[16,1,1408]{2,1,0:T(1,128)} %bitcast.6), calls=%async_computation.1 | async-start | bytes 180224 | tf_op jit(solution)/shard_map/all_to_all | solution.py:221
  34.4 1.2 %shard_map.81 = f32[208,512]{1,0:T(8,128)} custom-call(s32[1]{0:T(128)} %bitcast.me, f32[2048,256]{1,0:T(8,128)S(1)} %get-tuple-element.9.snaps, f32[1,2048]{1,0:T(1,128)S(1)} %get-tuple-element.10.final, f32[200,256]{1,0:T(8,128)S(1)} %get-tuple-element.11.vectors), custom_call_target="tpu_custom_call" | custom-call | tf_op jit(solution)/shard_map/pallas_call | solution.py:38
  35.6 4.4 %collective-permute-start = (f32[208,512]{1,0:T(8,128)}, f32[208,512]{1,0:T(8,128)S(1)}, u32[]{:S(2)}, u32[]{:S(2)}) collective-permute-start(f32[208,512]{1,0:T(8,128)} %shard_map.81), channel_id=1, source_target_pairs={{0,3},{1,0},{2,1},{3,2},{4,7},{5,4},{6,5},{7,6},{8,11},{9,8},{10,9... | collective-permute-start | bytes 1277960 | tf_op jit(solution)/shard_map/ppermute | solution.py:235
  39.9 0.4 shard_map.82.own
  40.4 0.0 copy-start
  40.4 0.0 copy-start.1
  40.4 0.0 collective-permute-done.1.arrived
  40.4 0.1 shard_map.84
  40.5 2.1 %collective-permute-start.2 = (f32[208,512]{1,0:T(8,128)S(1)}, f32[208,512]{1,0:T(8,128)S(1)}, u32[]{:S(2)}, u32[]{:S(2)}) collective-permute-start(f32[208,512]{1,0:T(8,128)S(1)} %shard_map.84), channel_id=1, source_target_pairs={{0,1},{1,2},{2,3},{3,0},{4,5},{5,6},{6,7},{7,4},{8,9},{9,10},{10,1... | collective-permute-start | bytes 1277960 | tf_op jit(solution)/shard_map/ppermute | solution.py:235
  42.5 0.0 all-to-all-done.1
  42.5 0.7 %shard_map.79 = f32[352,128]{1,0:T(8,128)} custom-call(f32[176,128]{1,0:T(8,128)S(1)} %bitcast.14), custom_call_target="tpu_custom_call" | custom-call | tf_op jit(solution)/shard_map/pallas_call | solution.py:38
  43.2 8.6 %all-to-all-start.2 = ((f32[32,1,1408]{2,1,0:T(1,128)}), f32[32,1,1408]{2,1,0:T(1,128)S(1)}, u32[]{:S(2)}, u32[]{:S(2)}) async-start(f32[32,1,1408]{2,1,0:T(1,128)} %bitcast.8), calls=%async_computation.2 | async-start | bytes 360448 | tf_op jit(solution)/shard_map/all_to_all | solution.py:221
  51.8 1.6 %shard_map.80.own = f32[208,512]{1,0:T(8,128)S(1)} custom-call(s32[1]{0:T(128)} %bitcast.me, f32[2048,256]{1,0:T(8,128)} %snaps.3, f32[1,2048]{1,0:T(1,128)} %bitcast.21, f32[200,256]{1,0:T(8,128)} %bitcast.19), custom_call_target="tpu_custom_call" | custom-call | tf_op jit(solution)/shard_map/pallas_call | solution.py:38
  53.4 0.0 collective-permute-done.from_right
  53.5 1.9 %collective-permute-done.2.from_left = f32[208,512]{1,0:T(8,128)S(1)} collective-permute-done((f32[208,512]{1,0:T(8,128)S(1)}, f32[208,512]{1,0:T(8,128)S(1)}, u32[]{:S(2)}, u32[]{:S(2)}) %collective-permute-start.2) | collective-permute-done | bytes 426016 | tf_op jit(solution)/shard_map/ppermute | solution.py:235
  55.4 0.0 copy-done
  55.4 0.0 copy-done.1
  55.4 1.4 %shard_map.85 = (f32[200,512]{1,0:T(8,128)}, f32[4,200]{1,0:T(4,128)S(1)}) custom-call(f32[208,512]{1,0:T(8,128)S(1)} %shard_map.80.own, f32[208,512]{1,0:T(8,128)S(1)} %collective-permute-done.from_right, f32[208,512]{1,0:T(8,128)S(1)} %collective-permute-done.2.from_left, f32[1,200]{1,0:T(1,128)S(1)} %bitcast.15, f32[200,200]{1,0:T(8,128)S(1)} %copy-done), custom_call_target="tpu_custom_call" | custom-call | tf_op jit(solution)/shard_map/pallas_call | solution.py:38
  56.8 0.5 all-to-all-done.2
  57.4 1.0 %shard_map.86 = f32[200,200]{1,0:T(8,128)} custom-call(f32[352,128]{1,0:T(8,128)S(1)} %bitcast.12, f32[4,200]{1,0:T(4,128)S(1)} %get-tuple-element.12.rows, f32[1,200]{1,0:T(1,128)S(1)} %bitcast.16), custom_call_target="tpu_custom_call" | custom-call | tf_op jit(solution)/shard_map/pallas_call | solution.py:38
Async XLA Ops:
  4.7 16.3 %all-to-all-start = ((f32[32,1,1408]{2,1,0:T(1,128)}), f32[32,1,1408]{2,1,0:T(1,128)S(1)}, u32[]{:S(2)}, u32[]{:S(2)}) async-start(f32[32,1,1408]{2,1,0:T(1,128)} %bitcast.4), calls=%async_computation | async-start | bytes 360448 | tf_op jit(solution)/shard_map/all_to_all | solution.py:221
  18.9 21.5 %collective-permute-start.1 = (f32[208,512]{1,0:T(8,128)}, f32[208,512]{1,0:T(8,128)S(1)}, u32[]{:S(2)}, u32[]{:S(2)}) collective-permute-start(f32[208,512]{1,0:T(8,128)} %shard_map.83), channel_id=1, source_target_pairs={{0,1},{1,2},{2,3},{3,0},{4,5},{5,6},{6,7},{7,4},{8,9},{9,10},{10,1... | collective-permute-start | bytes 1277960 | tf_op jit(solution)/shard_map/ppermute | solution.py:235
  21.7 20.9 %all-to-all-start.1 = ((f32[16,1,1408]{2,1,0:T(1,128)}), f32[16,1,1408]{2,1,0:T(1,128)S(1)}, u32[]{:S(2)}, u32[]{:S(2)}) async-start(f32[16,1,1408]{2,1,0:T(1,128)} %bitcast.6), calls=%async_computation.1 | async-start | bytes 180224 | tf_op jit(solution)/shard_map/all_to_all | solution.py:221
  35.6 17.9 %collective-permute-start = (f32[208,512]{1,0:T(8,128)}, f32[208,512]{1,0:T(8,128)S(1)}, u32[]{:S(2)}, u32[]{:S(2)}) collective-permute-start(f32[208,512]{1,0:T(8,128)} %shard_map.81), channel_id=1, source_target_pairs={{0,3},{1,0},{2,1},{3,2},{4,7},{5,4},{6,5},{7,6},{8,11},{9,8},{10,9... | collective-permute-start | bytes 1277960 | tf_op jit(solution)/shard_map/ppermute | solution.py:235
  40.4 15.0 %copy-start = (f32[200,200]{1,0:T(8,128)S(1)}, f32[200,200]{1,0:T(8,128)}, u32[]{:S(2)}) copy-start(f32[200,200]{1,0:T(8,128)} %eigen.1) | copy-start | bytes 480004
  40.4 15.0 %copy-start.1 = (f32[200]{0:T(256)S(1)}, f32[200]{0:T(256)}, u32[]{:S(2)}) copy-start(f32[200]{0:T(256)} %param.10) | copy-start | bytes 2404
  40.5 14.9 %collective-permute-start.2 = (f32[208,512]{1,0:T(8,128)S(1)}, f32[208,512]{1,0:T(8,128)S(1)}, u32[]{:S(2)}, u32[]{:S(2)}) collective-permute-start(f32[208,512]{1,0:T(8,128)S(1)} %shard_map.84), channel_id=1, source_target_pairs={{0,1},{1,2},{2,3},{3,0},{4,5},{5,6},{6,7},{7,4},{8,9},{9,10},{10,1... | collective-permute-start | bytes 1277960 | tf_op jit(solution)/shard_map/ppermute | solution.py:235
  43.2 14.1 %all-to-all-start.2 = ((f32[32,1,1408]{2,1,0:T(1,128)}), f32[32,1,1408]{2,1,0:T(1,128)S(1)}, u32[]{:S(2)}, u32[]{:S(2)}) async-start(f32[32,1,1408]{2,1,0:T(1,128)} %bitcast.8), calls=%async_computation.2 | async-start | bytes 360448 | tf_op jit(solution)/shard_map/all_to_all | solution.py:221

commit v5 on v4

--- a/solution.py
+++ b/solution.py
@@ -18,7 +18,6 @@
 LANES = 128
 BLOCKS = 4
 EXTRA = 2 * BLOCKS
-CHUNK = 512
 VMEM_GRANT = 16 << 20
 
 
@@ -75,23 +74,27 @@
 
 
 def term_kernel(
-    me, snaps, final, modes, vectors, packed, snaps_in, final_in, vectors_in, modes_in, sems
+    me, snaps, final, modes, vectors, packed, first_in, second_in, third_in, final_in, vectors_in, own_in, modes_in, sems
 ):
     rank, _ = vectors.shape
-    chunks = snaps.shape[0] // CHUNK
-    spans = [pl.ds(i * CHUNK, CHUNK) for i in range(chunks)]
+    points = own_in.shape[0]
+    held = (own_in, first_in, second_in, third_in)
+    spans = [
+        pl.ds(pl.multiple_of(lax.rem(me[0] + i, BLOCKS) * points, points), points)
+        for i in range(BLOCKS)
+    ]
     got_modes = [
-        pltpu.make_async_copy(modes.at[:, here], modes_in.at[:, here], sems.at[i])
+        pltpu.make_async_copy(modes.at[:, here], modes_in.at[:, pl.ds(i * points, points)], sems.at[i])
         for i, here in enumerate(spans)
     ]
     got_snaps = [
-        pltpu.make_async_copy(snaps.at[here, :], snaps_in.at[here, :], sems.at[chunks + i])
+        pltpu.make_async_copy(snaps.at[here, :], held[i], sems.at[BLOCKS + i])
         for i, here in enumerate(spans)
     ]
-    got_final = pltpu.make_async_copy(final, final_in, sems.at[2 * chunks])
-    got_vectors = pltpu.make_async_copy(vectors, vectors_in, sems.at[2 * chunks + 1])
+    got_final = pltpu.make_async_copy(final, final_in, sems.at[2 * BLOCKS])
+    got_vectors = pltpu.make_async_copy(vectors, vectors_in, sems.at[2 * BLOCKS + 1])
     got_final.start()
-    for i in range(chunks):
+    for i in range(BLOCKS):
         got_modes[i].start()
         got_snaps[i].start()
     got_vectors.start()
@@ -101,10 +104,10 @@
     for i, here in enumerate(spans):
         got_modes[i].wait()
         got_snaps[i].wait()
-        left, last = modes_in[:, here], final_in[:, here]
-        product = three_pass(split(left), split(snaps_in[here, :]), (1, 0))
+        left, last = modes_in[:, i * points : (i + 1) * points], final_in[:, here]
+        product = three_pass(split(left), split(held[i][...]), (1, 0))
         total = product if total is None else total + product
-        for j in range(0, CHUNK, LANES):
+        for j in range(0, points, LANES):
             column = left[:, j : j + LANES] * last[:, j : j + LANES]
             of_final = column if of_final is None else of_final + column
     got_vectors.wait()
@@ -144,7 +147,7 @@
     rank, points = vectors.shape[0], out.shape[1]
     owner = lax.rem(me[0] + distance, BLOCKS)
     here = pl.ds(pl.multiple_of(owner * points, points), points)
-    out[:rank, :], out[rank:, :] = shares_of(me[0], snaps[here, :], final[:, here], vectors[...])
+    out[:rank, :], out[rank:, :] = shares_of(me[0], snaps[...], final[:, here], vectors[...])
 
 
 def add_kernel(own, arrived, out):
@@ -238,13 +241,13 @@
     near_groups, far_groups = groups_of(NEAR, NEAR_FIRST), groups_of(FAR, FAR_FIRST)
     lines = rank + 2 * (rank - LANES + BLOCKS)
     size = lines // near
-    packed, snaps_in, final_in, vectors_in = call(
+    packed, *snaps_in, final_in, vectors_in = call(
         term_kernel,
         (
             f32(lines, LANES),
-            pltpu.VMEM(snapshots.shape, jnp.float32),
-            pltpu.VMEM((1, rows), jnp.float32),
-            pltpu.VMEM((rank, snapshots.shape[1]), jnp.float32),
+            *[f32(2 * half, snapshots.shape[1])] * (BLOCKS - 1),
+            f32(1, rows),
+            f32(rank, snapshots.shape[1]),
         ),
         me,
         snapshots,
@@ -254,8 +257,9 @@
         smem=1,
         hbm=(1, 2, 3, 4),
         scratch=(
+            pltpu.VMEM((2 * half, snapshots.shape[1]), jnp.float32),
             pltpu.VMEM((rank, rows), jnp.float32),
-            pltpu.SemaphoreType.DMA((2 * (rows // CHUNK) + 2,)),
+            pltpu.SemaphoreType.DMA((2 * BLOCKS + 2,)),
         ),
     )
     tiles = exchanged(packed, near_groups)
@@ -264,7 +268,7 @@
 
     def share_for(distance):
         kernel = functools.partial(share_kernel, distance=distance)
-        return call(kernel, share, me, snaps_in, final_in, vectors_in, smem=1)
+        return call(kernel, share, me, snaps_in[distance - 1], final_in, vectors_in, smem=1)
 
     two_right, left, one_right = share_for(2), share_for(3), share_for(1)
     from_left = sent(two_right, 1)

time: 58.8 us -> 58 us (0.986)
  Pallas kernels: 12.3 us -> 10.9 us
  waiting for transfers between devices: 2.68 us -> 3.72 us
    pallas_call x10, Pallas kernels: 12.3 us -> 10.9 us  [call(): pl.pallas_call(kernel, out_shape=outs, in_specs=specs, scratch_shapes=scr...]
    ppermute x3, waiting for transfers between devices: 1.94 us -> 2.55 us  [sent(): lax.ppermute(value, 'tm', [(i, (i + distance) % blocks) for i in range(bl...]
  transfers between devices with their start and end apart: 6 -> 6, of which waited for: 3 -> 3; matrix products, arithmetic and copies ran while one was open for 0% -> 0% of each run, Pallas kernels for 13% -> 10%
where the time goes in v5:
time: 58 us; the launch traced here: 57.5 us
  starting transfers between devices  42.2 us (73%)
  Pallas kernels  10.9 us (19%)
  waiting for transfers between devices  3.72 us (6%)
  between operations  0.75 us (1%)
    all_to_all x3, starting transfers between devices, exchanged(): lax.all_to_all(pieces, ALL, split_axis=0, concat_axis=0, tiled=True, axis...  34 us
    pallas_call x10, Pallas kernels, call(): pl.pallas_call(kernel, out_shape=outs, in_specs=specs, scratch_shapes=scr...  10.9 us
    ppermute x3, starting transfers between devices, sent(): lax.ppermute(value, 'tm', [(i, (i + distance) % blocks) for i in range(bl...  8.21 us
    ppermute x3, waiting for transfers between devices, sent(): lax.ppermute(value, 'tm', [(i, (i + distance) % blocks) for i in range(bl...  2.55 us
    all_to_all x3, waiting for transfers between devices, exchanged(): lax.all_to_all(pieces, ALL, split_axis=0, concat_axis=0, tiled=True, axis...  1.16 us
  transfers between devices with their start and end apart: 6, of which 3 were waited for; matrix products, arithmetic and copies ran while one was open for 0% of the time, Pallas kernels for 10%

profile of v5, /device:TPU:1, one launch (start us, length us, event | category | flops | bytes accessed | tf_op | source)
XLA Modules:
  0.0 57.5 jit_solution(7421730504924039715)
XLA Ops:
  0.6 4.1 %shard_map.77 = (f32[352,128]{1,0:T(8,128)}, f32[512,256]{1,0:T(8,128)S(1)}, f32[512,256]{1,0:T(8,128)S(1)}, f32[512,256]{1,0:T(8,128)S(1)}, f32[1,2048]{1,0:T(1,128)S(1)}, /*index=5*/f32[200,256]{1,0:T(8,128)S(1)}) custom-call(s32[1]{0:T(128)} %bitcast.me, f32[2048,256]{1,0:T(8,128)} %snaps.3, f32[1,2048]{1,0:T(1,128)} %bitcast.20, f32[200,2048]{1,0:T(8,128)} %bitcast.17, ...), custom_call_target="tpu_custom_call" | custom-call | tf_op jit(solution)/shard_map/pallas_call | solution.py:37
  4.8 13.0 %all-to-all-start = ((f32[32,1,1408]{2,1,0:T(1,128)}), f32[32,1,1408]{2,1,0:T(1,128)S(1)}, u32[]{:S(2)}, u32[]{:S(2)}) async-start(f32[32,1,1408]{2,1,0:T(1,128)} %bitcast.4), calls=%async_computation | async-start | bytes 360448 | tf_op jit(solution)/shard_map/all_to_all | solution.py:224
  17.8 0.4 shard_map.83
  18.2 1.9 %collective-permute-start.1 = (f32[208,512]{1,0:T(8,128)S(1)}, f32[208,512]{1,0:T(8,128)S(1)}, u32[]{:S(2)}, u32[]{:S(2)}) collective-permute-start(f32[208,512]{1,0:T(8,128)S(1)} %shard_map.83), channel_id=1, source_target_pairs={{0,1},{1,2},{2,3},{3,0},{4,5},{5,6},{6,7},{7,4},{8,9},{9,10},{10,1... | collective-permute-start | bytes 1277960 | tf_op jit(solution)/shard_map/ppermute | solution.py:238
  20.1 1.0 %all-to-all-done = f32[32,1,1408]{2,1,0:T(1,128)S(1)} async-done(((f32[32,1,1408]{2,1,0:T(1,128)}), f32[32,1,1408]{2,1,0:T(1,128)S(1)}, u32[]{:S(2)}, u32[]{:S(2)}) %all-to-all-start) | async-done | bytes 180256 | tf_op jit(solution)/shard_map/all_to_all | solution.py:224
  21.1 0.7 %shard_map.78 = f32[176,128]{1,0:T(8,128)} custom-call(f32[352,128]{1,0:T(8,128)S(1)} %bitcast.13), custom_call_target="tpu_custom_call" | custom-call | tf_op jit(solution)/shard_map/pallas_call | solution.py:37
  21.8 12.7 %all-to-all-start.1 = ((f32[16,1,1408]{2,1,0:T(1,128)}), f32[16,1,1408]{2,1,0:T(1,128)S(1)}, u32[]{:S(2)}, u32[]{:S(2)}) async-start(f32[16,1,1408]{2,1,0:T(1,128)} %bitcast.6), calls=%async_computation.1 | async-start | bytes 180224 | tf_op jit(solution)/shard_map/all_to_all | solution.py:224
  34.5 0.4 shard_map.81
  34.9 4.2 %collective-permute-start = (f32[208,512]{1,0:T(8,128)S(1)}, f32[208,512]{1,0:T(8,128)S(1)}, u32[]{:S(2)}, u32[]{:S(2)}) collective-permute-start(f32[208,512]{1,0:T(8,128)S(1)} %shard_map.81), channel_id=1, source_target_pairs={{0,3},{1,0},{2,1},{3,2},{4,7},{5,4},{6,5},{7,6},{8,11},{9,8},{10,9... | collective-permute-start | bytes 1277960 | tf_op jit(solution)/shard_map/ppermute | solution.py:238
  39.1 0.4 shard_map.82.own
  39.6 0.0 copy-start
  39.6 0.0 copy-start.1
  39.6 0.0 collective-permute-done.1.arrived
  39.6 0.1 shard_map.84
  39.7 2.1 %collective-permute-start.2 = (f32[208,512]{1,0:T(8,128)S(1)}, f32[208,512]{1,0:T(8,128)S(1)}, u32[]{:S(2)}, u32[]{:S(2)}) collective-permute-start(f32[208,512]{1,0:T(8,128)S(1)} %shard_map.84), channel_id=1, source_target_pairs={{0,1},{1,2},{2,3},{3,0},{4,5},{5,6},{6,7},{7,4},{8,9},{9,10},{10,1... | collective-permute-start | bytes 1277960 | tf_op jit(solution)/shard_map/ppermute | solution.py:238
  41.7 0.0 all-to-all-done.1
  41.7 0.7 %shard_map.79 = f32[352,128]{1,0:T(8,128)} custom-call(f32[176,128]{1,0:T(8,128)S(1)} %bitcast.14), custom_call_target="tpu_custom_call" | custom-call | tf_op jit(solution)/shard_map/pallas_call | solution.py:37
  42.4 8.3 %all-to-all-start.2 = ((f32[32,1,1408]{2,1,0:T(1,128)}), f32[32,1,1408]{2,1,0:T(1,128)S(1)}, u32[]{:S(2)}, u32[]{:S(2)}) async-start(f32[32,1,1408]{2,1,0:T(1,128)} %bitcast.8), calls=%async_computation.2 | async-start | bytes 360448 | tf_op jit(solution)/shard_map/all_to_all | solution.py:224
  50.7 1.6 %shard_map.80.own = f32[208,512]{1,0:T(8,128)S(1)} custom-call(s32[1]{0:T(128)} %bitcast.me, f32[2048,256]{1,0:T(8,128)} %snaps.3, f32[1,2048]{1,0:T(1,128)} %bitcast.21, f32[200,256]{1,0:T(8,128)} %bitcast.19), custom_call_target="tpu_custom_call" | custom-call | tf_op jit(solution)/shard_map/pallas_call | solution.py:37
  52.3 0.0 collective-permute-done.from_right
  52.3 2.5 %collective-permute-done.2.from_left = f32[208,512]{1,0:T(8,128)S(1)} collective-permute-done((f32[208,512]{1,0:T(8,128)S(1)}, f32[208,512]{1,0:T(8,128)S(1)}, u32[]{:S(2)}, u32[]{:S(2)}) %collective-permute-start.2) | collective-permute-done | bytes 426016 | tf_op jit(solution)/shard_map/ppermute | solution.py:238
  54.9 0.0 copy-done
  54.9 0.0 copy-done.1
  54.9 1.4 %shard_map.85 = (f32[200,512]{1,0:T(8,128)}, f32[4,200]{1,0:T(4,128)S(1)}) custom-call(f32[208,512]{1,0:T(8,128)S(1)} %shard_map.80.own, f32[208,512]{1,0:T(8,128)S(1)} %collective-permute-done.from_right, f32[208,512]{1,0:T(8,128)S(1)} %collective-permute-done.2.from_left, f32[1,200]{1,0:T(1,128)S(1)} %bitcast.15, f32[200,200]{1,0:T(8,128)S(1)} %copy-done), custom_call_target="tpu_custom_call" | custom-call | tf_op jit(solution)/shard_map/pallas_call | solution.py:37
  56.3 0.2 all-to-all-done.2
  56.6 1.0 %shard_map.86 = f32[200,200]{1,0:T(8,128)} custom-call(f32[352,128]{1,0:T(8,128)S(1)} %bitcast.12, f32[4,200]{1,0:T(4,128)S(1)} %get-tuple-element.16.rows, f32[1,200]{1,0:T(1,128)S(1)} %bitcast.16), custom_call_target="tpu_custom_call" | custom-call | tf_op jit(solution)/shard_map/pallas_call | solution.py:37
Async XLA Ops:
  4.8 16.3 %all-to-all-start = ((f32[32,1,1408]{2,1,0:T(1,128)}), f32[32,1,1408]{2,1,0:T(1,128)S(1)}, u32[]{:S(2)}, u32[]{:S(2)}) async-start(f32[32,1,1408]{2,1,0:T(1,128)} %bitcast.4), calls=%async_computation | async-start | bytes 360448 | tf_op jit(solution)/shard_map/all_to_all | solution.py:224
  18.2 21.4 %collective-permute-start.1 = (f32[208,512]{1,0:T(8,128)S(1)}, f32[208,512]{1,0:T(8,128)S(1)}, u32[]{:S(2)}, u32[]{:S(2)}) collective-permute-start(f32[208,512]{1,0:T(8,128)S(1)} %shard_map.83), channel_id=1, source_target_pairs={{0,1},{1,2},{2,3},{3,0},{4,5},{5,6},{6,7},{7,4},{8,9},{9,10},{10,1... | collective-permute-start | bytes 1277960 | tf_op jit(solution)/shard_map/ppermute | solution.py:238
  21.8 20.0 %all-to-all-start.1 = ((f32[16,1,1408]{2,1,0:T(1,128)}), f32[16,1,1408]{2,1,0:T(1,128)S(1)}, u32[]{:S(2)}, u32[]{:S(2)}) async-start(f32[16,1,1408]{2,1,0:T(1,128)} %bitcast.6), calls=%async_computation.1 | async-start | bytes 180224 | tf_op jit(solution)/shard_map/all_to_all | solution.py:224
  34.9 17.4 %collective-permute-start = (f32[208,512]{1,0:T(8,128)S(1)}, f32[208,512]{1,0:T(8,128)S(1)}, u32[]{:S(2)}, u32[]{:S(2)}) collective-permute-start(f32[208,512]{1,0:T(8,128)S(1)} %shard_map.81), channel_id=1, source_target_pairs={{0,3},{1,0},{2,1},{3,2},{4,7},{5,4},{6,5},{7,6},{8,11},{9,8},{10,9... | collective-permute-start | bytes 1277960 | tf_op jit(solution)/shard_map/ppermute | solution.py:238
  39.6 15.3 %copy-start = (f32[200,200]{1,0:T(8,128)S(1)}, f32[200,200]{1,0:T(8,128)}, u32[]{:S(2)}) copy-start(f32[200,200]{1,0:T(8,128)} %eigen.1) | copy-start | bytes 480004
  39.6 15.3 %copy-start.1 = (f32[200]{0:T(256)S(1)}, f32[200]{0:T(256)}, u32[]{:S(2)}) copy-start(f32[200]{0:T(256)} %param.10) | copy-start | bytes 2404
  39.7 15.2 %collective-permute-start.2 = (f32[208,512]{1,0:T(8,128)S(1)}, f32[208,512]{1,0:T(8,128)S(1)}, u32[]{:S(2)}, u32[]{:S(2)}) collective-permute-start(f32[208,512]{1,0:T(8,128)S(1)} %shard_map.84), channel_id=1, source_target_pairs={{0,1},{1,2},{2,3},{3,0},{4,5},{5,6},{6,7},{7,4},{8,9},{9,10},{10,1... | collective-permute-start | bytes 1277960 | tf_op jit(solution)/shard_map/ppermute | solution.py:238
  42.4 14.1 %all-to-all-start.2 = ((f32[32,1,1408]{2,1,0:T(1,128)}), f32[32,1,1408]{2,1,0:T(1,128)S(1)}, u32[]{:S(2)}, u32[]{:S(2)}) async-start(f32[32,1,1408]{2,1,0:T(1,128)} %bitcast.8), calls=%async_computation.2 | async-start | bytes 360448 | tf_op jit(solution)/shard_map/all_to_all | solution.py:224

commit v6 on v5

--- a/solution.py
+++ b/solution.py
@@ -59,6 +59,10 @@
     return dot(a_high, b_high) + (dot(a_high, b_low) + dot(a_low, b_high))
 
 
+def block_and_step(place):
+    return lax.rem(place, BLOCKS), 1 + (BLOCKS - 2) * lax.div(place, BLOCKS)
+
+
 def shifted(vectors):
     lane = lax.broadcasted_iota(jnp.int32, vectors.shape, 1)
     return jnp.where(lane == 0, 0.0, pltpu.roll(vectors, 1, 1))
@@ -74,13 +78,14 @@
 
 
 def term_kernel(
-    me, snaps, final, modes, vectors, packed, first_in, second_in, third_in, final_in, vectors_in, own_in, modes_in, sems
+    place, snaps, final, modes, vectors, packed, first_in, second_in, third_in, final_in, vectors_in, own_in, modes_in, sems
 ):
     rank, _ = vectors.shape
     points = own_in.shape[0]
+    block, step = block_and_step(place[0])
     held = (own_in, first_in, second_in, third_in)
     spans = [
-        pl.ds(pl.multiple_of(lax.rem(me[0] + i, BLOCKS) * points, points), points)
+        pl.ds(pl.multiple_of(lax.rem(block + i * step, BLOCKS) * points, points), points)
         for i in range(BLOCKS)
     ]
     got_modes = [
@@ -113,12 +118,12 @@
     got_vectors.wait()
     whole = three_pass(split(total), split(shifted(vectors_in[...])))
     of_final = jnp.sum(of_final, axis=1, keepdims=True)
-    first = jnp.where(me[0] == 0, of_final, total[:, :1])
+    first = jnp.where(block == 0, of_final, total[:, :1])
     packed[:rank, :] = whole[:, :LANES]
     rest = rank - LANES
     tail = jnp.pad(whole[:, LANES:], ((0, 0), (0, LANES - rest)))
     lane = lax.broadcasted_iota(jnp.int32, tail.shape, 1)
-    tail = jnp.where(lane == rest + me[0], first, tail)
+    tail = jnp.where(lane == rest + block, first, tail)
     tail = jnp.pad(tail, ((0, 2 * LANES - rank), (0, 0)))
     used = rest + BLOCKS
     for i in range(2):
@@ -143,11 +148,12 @@
     return block[:rank], extra
 
 
-def share_kernel(me, snaps, final, vectors, out, *, distance):
+def share_kernel(place, snaps, final, vectors, out, *, distance):
     rank, points = vectors.shape[0], out.shape[1]
-    owner = lax.rem(me[0] + distance, BLOCKS)
+    block, step = block_and_step(place[0])
+    owner = lax.rem(block + distance * step, BLOCKS)
     here = pl.ds(pl.multiple_of(owner * points, points), points)
-    out[:rank, :], out[rank:, :] = shares_of(me[0], snaps[...], final[:, here], vectors[...])
+    out[:rank, :], out[rank:, :] = shares_of(block, snaps[...], final[:, here], vectors[...])
 
 
 def add_kernel(own, arrived, out):
@@ -162,9 +168,10 @@
         out[i * size : (i + 1) * size, :] = total
 
 
-def own_share_kernel(me, snaps, final, vectors, out, snaps_in, final_in, vectors_in, sems):
+def own_share_kernel(place, snaps, final, vectors, out, snaps_in, final_in, vectors_in, sems):
     rank, points = vectors.shape[0], out.shape[1]
-    here = pl.ds(pl.multiple_of(me[0] * points, points), points)
+    block, _ = block_and_step(place[0])
+    here = pl.ds(pl.multiple_of(block * points, points), points)
     copies = (
         pltpu.make_async_copy(vectors, vectors_in, sems.at[0]),
         pltpu.make_async_copy(snaps.at[here, :], snaps_in, sems.at[1]),
@@ -174,7 +181,7 @@
         copy.start()
     for copy in copies:
         copy.wait()
-    out[:rank, :], out[rank:, :] = shares_of(me[0], snaps_in[...], final_in[...], vectors_in[...])
+    out[:rank, :], out[rank:, :] = shares_of(block, snaps_in[...], final_in[...], vectors_in[...])
 
 
 def dmd_kernel(own, from_right, from_left, sing, eigen, out, rows):
@@ -231,11 +238,19 @@
     blocks = lax.axis_size("tm")
     rows, rank = snapshots.shape[0], right_vectors.shape[1]
     half = rows // (2 * blocks)
-    me = lax.axis_index("tm").astype(jnp.int32)[None]
+    place = lax.axis_index(("core", "tm")).astype(jnp.int32)[None]
     sing = inverse_sing[None, :]
 
     def sent(value, distance):
-        return lax.ppermute(value, "tm", [(i, (i + distance) % blocks) for i in range(blocks)])
+        return lax.ppermute(
+            value,
+            ("core", "tm"),
+            [
+                (core * blocks + i, core * blocks + (i + distance * (1 - 2 * core)) % blocks)
+                for core in range(lax.axis_size("core"))
+                for i in range(blocks)
+            ],
+        )
 
     near, far = lax.axis_size(NEAR), lax.axis_size(FAR)
     near_groups, far_groups = groups_of(NEAR, NEAR_FIRST), groups_of(FAR, FAR_FIRST)
@@ -249,7 +264,7 @@
             f32(1, rows),
             f32(rank, snapshots.shape[1]),
         ),
-        me,
+        place,
         snapshots,
         final_snapshot[None, :],
         pod_modes.T,
@@ -268,7 +283,7 @@
 
     def share_for(distance):
         kernel = functools.partial(share_kernel, distance=distance)
-        return call(kernel, share, me, snaps_in[distance - 1], final_in, vectors_in, smem=1)
+        return call(kernel, share, place, snaps_in[distance - 1], final_in, vectors_in, smem=1)
 
     two_right, left, one_right = share_for(2), share_for(3), share_for(1)
     from_left = sent(two_right, 1)
@@ -284,7 +299,7 @@
     own = call(
         own_share_kernel,
         share,
-        me,
+        place,
         snapshots,
         final_snapshot[None, :],
         right_vectors.T,

time: 58 us -> 55.5 us (0.957)
  waiting for transfers between devices: 3.72 us -> 0.92 us
    ppermute x3, waiting for transfers between devices: 2.55 us -> 0.01 us  [sent(): lax.ppermute(value, ('core', 'tm'), [(core * blocks + i, core * blocks +...]
    ppermute x3, starting transfers between devices: 8.21 us -> 8.81 us  [sent(): lax.ppermute(value, ('core', 'tm'), [(core * blocks + i, core * blocks +...]
  transfers between devices with their start and end apart: 6 -> 6, of which waited for: 3 -> 2; matrix products, arithmetic and copies ran while one was open for 0% -> 0% of each run, Pallas kernels for 10% -> 11%
where the time goes in v6:
time: 55.5 us; the launch traced here: 55 us
  starting transfers between devices  42.4 us (76%)
  Pallas kernels  10.9 us (20%)
  waiting for transfers between devices  0.92 us (2%)
  between operations  0.78 us (1%)
    all_to_all x3, starting transfers between devices, exchanged(): lax.all_to_all(pieces, ALL, split_axis=0, concat_axis=0, tiled=True, axis...  33.6 us
    pallas_call x10, Pallas kernels, call(): pl.pallas_call(kernel, out_shape=outs, in_specs=specs, scratch_shapes=scr...  10.9 us
    ppermute x3, starting transfers between devices, sent(): lax.ppermute(value, ('core', 'tm'), [(core * blocks + i, core * blocks +...  8.81 us
  transfers between devices with their start and end apart: 6, of which 2 were waited for; matrix products, arithmetic and copies ran while one was open for 0% of the time, Pallas kernels for 11%

profile of v6, /device:TPU:1, one launch (start us, length us, event | category | flops | bytes accessed | tf_op | source)
XLA Modules:
  0.0 55.0 jit_solution(15628084619472711115)
XLA Ops:
  0.6 4.1 %shard_map.77 = (f32[352,128]{1,0:T(8,128)}, f32[512,256]{1,0:T(8,128)S(1)}, f32[512,256]{1,0:T(8,128)S(1)}, f32[512,256]{1,0:T(8,128)S(1)}, f32[1,2048]{1,0:T(1,128)S(1)}, /*index=5*/f32[200,256]{1,0:T(8,128)S(1)}) custom-call(s32[1]{0:T(128)} %bitcast.place, f32[2048,256]{1,0:T(8,128)} %snaps.3, f32[1,2048]{1,0:T(1,128)} %bitcast.20, ...), custom_call_target="tpu_custom_call" | custom-call | tf_op jit(solution)/shard_map/pallas_call | solution.py:37
  4.8 13.0 %all-to-all-start = ((f32[32,1,1408]{2,1,0:T(1,128)}), f32[32,1,1408]{2,1,0:T(1,128)S(1)}, u32[]{:S(2)}, u32[]{:S(2)}) async-start(f32[32,1,1408]{2,1,0:T(1,128)} %bitcast.4), calls=%async_computation | async-start | bytes 360448 | tf_op jit(solution)/shard_map/all_to_all | solution.py:231
  17.8 0.4 shard_map.83
  18.2 2.2 %collective-permute-start.1 = (f32[208,512]{1,0:T(8,128)S(1)}, f32[208,512]{1,0:T(8,128)S(1)}, u32[]{:S(2)}, u32[]{:S(2)}) collective-permute-start(f32[208,512]{1,0:T(8,128)S(1)} %shard_map.83), channel_id=1, source_target_pairs={{0,1},{1,2},{2,3},{3,0},{4,7},{5,4},{6,5},{7,6},{8,9},{9,10},{10,1... | collective-permute-start | bytes 1277960 | tf_op jit(solution)/shard_map/ppermute | solution.py:245
  20.4 0.7 %all-to-all-done = f32[32,1,1408]{2,1,0:T(1,128)S(1)} async-done(((f32[32,1,1408]{2,1,0:T(1,128)}), f32[32,1,1408]{2,1,0:T(1,128)S(1)}, u32[]{:S(2)}, u32[]{:S(2)}) %all-to-all-start) | async-done | bytes 180256 | tf_op jit(solution)/shard_map/all_to_all | solution.py:231
  21.1 0.7 %shard_map.78 = f32[176,128]{1,0:T(8,128)} custom-call(f32[352,128]{1,0:T(8,128)S(1)} %bitcast.13), custom_call_target="tpu_custom_call" | custom-call | tf_op jit(solution)/shard_map/pallas_call | solution.py:37
  21.8 12.7 %all-to-all-start.1 = ((f32[16,1,1408]{2,1,0:T(1,128)}), f32[16,1,1408]{2,1,0:T(1,128)S(1)}, u32[]{:S(2)}, u32[]{:S(2)}) async-start(f32[16,1,1408]{2,1,0:T(1,128)} %bitcast.6), calls=%async_computation.1 | async-start | bytes 180224 | tf_op jit(solution)/shard_map/all_to_all | solution.py:231
  34.5 0.4 shard_map.81
  34.9 2.9 %collective-permute-start = (f32[208,512]{1,0:T(8,128)S(1)}, f32[208,512]{1,0:T(8,128)S(1)}, u32[]{:S(2)}, u32[]{:S(2)}) collective-permute-start(f32[208,512]{1,0:T(8,128)S(1)} %shard_map.81), channel_id=1, source_target_pairs={{0,3},{1,0},{2,1},{3,2},{4,5},{5,6},{6,7},{7,4},{8,11},{9,8},{10,9... | collective-permute-start | bytes 1277960 | tf_op jit(solution)/shard_map/ppermute | solution.py:245
  37.8 0.4 shard_map.82.own
  38.3 0.0 copy-start
  38.3 0.0 copy-start.1
  38.3 0.0 collective-permute-done.1.arrived
  38.3 0.1 shard_map.84
  38.4 3.7 %collective-permute-start.2 = (f32[208,512]{1,0:T(8,128)S(1)}, f32[208,512]{1,0:T(8,128)S(1)}, u32[]{:S(2)}, u32[]{:S(2)}) collective-permute-start(f32[208,512]{1,0:T(8,128)S(1)} %shard_map.84), channel_id=1, source_target_pairs={{0,1},{1,2},{2,3},{3,0},{4,7},{5,4},{6,5},{7,6},{8,9},{9,10},{10,1... | collective-permute-start | bytes 1277960 | tf_op jit(solution)/shard_map/ppermute | solution.py:245
  42.1 0.0 all-to-all-done.1
  42.1 0.7 %shard_map.79 = f32[352,128]{1,0:T(8,128)} custom-call(f32[176,128]{1,0:T(8,128)S(1)} %bitcast.14), custom_call_target="tpu_custom_call" | custom-call | tf_op jit(solution)/shard_map/pallas_call | solution.py:37
  42.8 7.9 %all-to-all-start.2 = ((f32[32,1,1408]{2,1,0:T(1,128)}), f32[32,1,1408]{2,1,0:T(1,128)S(1)}, u32[]{:S(2)}, u32[]{:S(2)}) async-start(f32[32,1,1408]{2,1,0:T(1,128)} %bitcast.8), calls=%async_computation.2 | async-start | bytes 360448 | tf_op jit(solution)/shard_map/all_to_all | solution.py:231
  50.7 1.6 %shard_map.80.own = f32[208,512]{1,0:T(8,128)S(1)} custom-call(s32[1]{0:T(128)} %bitcast.place, f32[2048,256]{1,0:T(8,128)} %snaps.3, f32[1,2048]{1,0:T(1,128)} %bitcast.21, f32[200,256]{1,0:T(8,128)} %bitcast.19), custom_call_target="tpu_custom_call" | custom-call | tf_op jit(solution)/shard_map/pallas_call | solution.py:37
  52.3 0.0 collective-permute-done.from_right
  52.4 0.0 collective-permute-done.2.from_left
  52.4 0.0 copy-done
  52.4 0.0 copy-done.1
  52.4 1.4 %shard_map.85 = (f32[200,512]{1,0:T(8,128)}, f32[4,200]{1,0:T(4,128)S(1)}) custom-call(f32[208,512]{1,0:T(8,128)S(1)} %shard_map.80.own, f32[208,512]{1,0:T(8,128)S(1)} %collective-permute-done.from_right, f32[208,512]{1,0:T(8,128)S(1)} %collective-permute-done.2.from_left, f32[1,200]{1,0:T(1,128)S(1)} %bitcast.15, f32[200,200]{1,0:T(8,128)S(1)} %copy-done), custom_call_target="tpu_custom_call" | custom-call | tf_op jit(solution)/shard_map/pallas_call | solution.py:37
  53.8 0.2 all-to-all-done.2
  54.0 1.0 %shard_map.86 = f32[200,200]{1,0:T(8,128)} custom-call(f32[352,128]{1,0:T(8,128)S(1)} %bitcast.12, f32[4,200]{1,0:T(4,128)S(1)} %get-tuple-element.16.rows, f32[1,200]{1,0:T(1,128)S(1)} %bitcast.16), custom_call_target="tpu_custom_call" | custom-call | tf_op jit(solution)/shard_map/pallas_call | solution.py:37
Async XLA Ops:
  4.8 16.3 %all-to-all-start = ((f32[32,1,1408]{2,1,0:T(1,128)}), f32[32,1,1408]{2,1,0:T(1,128)S(1)}, u32[]{:S(2)}, u32[]{:S(2)}) async-start(f32[32,1,1408]{2,1,0:T(1,128)} %bitcast.4), calls=%async_computation | async-start | bytes 360448 | tf_op jit(solution)/shard_map/all_to_all | solution.py:231
  18.2 20.1 %collective-permute-start.1 = (f32[208,512]{1,0:T(8,128)S(1)}, f32[208,512]{1,0:T(8,128)S(1)}, u32[]{:S(2)}, u32[]{:S(2)}) collective-permute-start(f32[208,512]{1,0:T(8,128)S(1)} %shard_map.83), channel_id=1, source_target_pairs={{0,1},{1,2},{2,3},{3,0},{4,7},{5,4},{6,5},{7,6},{8,9},{9,10},{10,1... | collective-permute-start | bytes 1277960 | tf_op jit(solution)/shard_map/ppermute | solution.py:245
  21.8 20.3 %all-to-all-start.1 = ((f32[16,1,1408]{2,1,0:T(1,128)}), f32[16,1,1408]{2,1,0:T(1,128)S(1)}, u32[]{:S(2)}, u32[]{:S(2)}) async-start(f32[16,1,1408]{2,1,0:T(1,128)} %bitcast.6), calls=%async_computation.1 | async-start | bytes 180224 | tf_op jit(solution)/shard_map/all_to_all | solution.py:231
  34.9 17.4 %collective-permute-start = (f32[208,512]{1,0:T(8,128)S(1)}, f32[208,512]{1,0:T(8,128)S(1)}, u32[]{:S(2)}, u32[]{:S(2)}) collective-permute-start(f32[208,512]{1,0:T(8,128)S(1)} %shard_map.81), channel_id=1, source_target_pairs={{0,3},{1,0},{2,1},{3,2},{4,5},{5,6},{6,7},{7,4},{8,11},{9,8},{10,9... | collective-permute-start | bytes 1277960 | tf_op jit(solution)/shard_map/ppermute | solution.py:245
  38.3 14.1 %copy-start = (f32[200,200]{1,0:T(8,128)S(1)}, f32[200,200]{1,0:T(8,128)}, u32[]{:S(2)}) copy-start(f32[200,200]{1,0:T(8,128)} %eigen.1) | copy-start | bytes 480004
  38.3 14.1 %copy-start.1 = (f32[200]{0:T(256)S(1)}, f32[200]{0:T(256)}, u32[]{:S(2)}) copy-start(f32[200]{0:T(256)} %param.10) | copy-start | bytes 2404
  38.4 14.0 %collective-permute-start.2 = (f32[208,512]{1,0:T(8,128)S(1)}, f32[208,512]{1,0:T(8,128)S(1)}, u32[]{:S(2)}, u32[]{:S(2)}) collective-permute-start(f32[208,512]{1,0:T(8,128)S(1)} %shard_map.84), channel_id=1, source_target_pairs={{0,1},{1,2},{2,3},{3,0},{4,7},{5,4},{6,5},{7,6},{8,9},{9,10},{10,1... | collective-permute-start | bytes 1277960 | tf_op jit(solution)/shard_map/ppermute | solution.py:245
  42.8 11.3 %all-to-all-start.2 = ((f32[32,1,1408]{2,1,0:T(1,128)}), f32[32,1,1408]{2,1,0:T(1,128)S(1)}, u32[]{:S(2)}, u32[]{:S(2)}) async-start(f32[32,1,1408]{2,1,0:T(1,128)} %bitcast.8), calls=%async_computation.2 | async-start | bytes 360448 | tf_op jit(solution)/shard_map/all_to_all | solution.py:231

commit v7 on v6

--- a/solution.py
+++ b/solution.py
@@ -13,8 +13,8 @@
 ALL = (*SPACE, "tm")
 NEAR = ("y_near", "z_near", "core", "tm")
 FAR = ("y_far", "z_far")
-NEAR_FIRST = (1, 1, 1, 2)
-FAR_FIRST = (2, 3)
+NEAR_FIRST = (0, 1, 1, 2)
+FAR_FIRST = (3, 3)
 LANES = 128
 BLOCKS = 4
 EXTRA = 2 * BLOCKS
@@ -98,13 +98,15 @@
     ]
     got_final = pltpu.make_async_copy(final, final_in, sems.at[2 * BLOCKS])
     got_vectors = pltpu.make_async_copy(vectors, vectors_in, sems.at[2 * BLOCKS + 1])
+    got_vectors.start()
     got_final.start()
     for i in range(BLOCKS):
         got_modes[i].start()
         got_snaps[i].start()
-    got_vectors.start()
 
     total = of_final = None
+    got_vectors.wait()
+    right = split(shifted(vectors_in[...]))
     got_final.wait()
     for i, here in enumerate(spans):
         got_modes[i].wait()
@@ -115,8 +117,7 @@
         for j in range(0, points, LANES):
             column = left[:, j : j + LANES] * last[:, j : j + LANES]
             of_final = column if of_final is None else of_final + column
-    got_vectors.wait()
-    whole = three_pass(split(total), split(shifted(vectors_in[...])))
+    whole = three_pass(split(total), right)
     of_final = jnp.sum(of_final, axis=1, keepdims=True)
     first = jnp.where(block == 0, of_final, total[:, :1])
     packed[:rank, :] = whole[:, :LANES]
@@ -199,21 +200,16 @@
     rank = out.shape[0]
     rest = rank - LANES
     used = rest + BLOCKS
-    first = jnp.concatenate(
-        [
-            packed[rank + rest : rank + used, :],
-            packed[rank + used + rest : rank + 2 * used, :][:, :rest],
-        ],
-        axis=1,
-    )
-    term = three_pass(split(first), split(rows[...]), (0, 0))
     scale = sing[...]
-    out[:, :LANES] = (packed[:rank, :] + term[:, :LANES]) * scale[:, :LANES]
     for i, size in ((0, LANES), (1, rest)):
-        tail = packed[rank + i * used : rank + i * used + rest, :]
-        turn = jnp.pad(tail, ((0, LANES - rest), (0, 0))).T[:size, :rest]
+        tail = packed[rank + i * used : rank + (i + 1) * used, :]
+        turn = jnp.pad(tail, ((0, LANES - used), (0, 0))).T[:size]
+        term = turn[:, rest : rest + 1] * rows[:1, :]
+        for j in range(1, BLOCKS):
+            term = term + turn[:, rest + j : rest + j + 1] * rows[j : j + 1, :]
         here = slice(i * LANES, i * LANES + size)
-        out[here, LANES:] = (turn + term[here, LANES:]) * scale[:, LANES:]
+        out[here, :LANES] = (packed[here, :] + term[:, :LANES]) * scale[:, :LANES]
+        out[here, LANES:] = (turn[:, :rest] + term[:, LANES:]) * scale[:, LANES:]
 
 
 def groups_of(axes, first):

time: 55.5 us -> 54.7 us (0.986)
  starting transfers between devices: 42.4 us -> 39.8 us
  waiting for transfers between devices: 0.92 us -> 2.94 us
    all_to_all x3, starting transfers between devices: 33.6 us -> 31 us  [exchanged(): lax.all_to_all(pieces, ALL, split_axis=0, concat_axis=0, tiled=True, axis...]
    all_to_all x3, waiting for transfers between devices: 0.91 us -> 2.93 us  [exchanged(): lax.all_to_all(pieces, ALL, split_axis=0, concat_axis=0, tiled=True, axis...]
where the time goes in v7:
time: 54.7 us; the launch traced here: 54.3 us
  starting transfers between devices  39.8 us (73%)
  Pallas kernels  10.8 us (20%)
  waiting for transfers between devices  2.94 us (5%)
  between operations  0.77 us (1%)
    all_to_all x3, starting transfers between devices, exchanged(): lax.all_to_all(pieces, ALL, split_axis=0, concat_axis=0, tiled=True, axis...  31 us
    pallas_call x10, Pallas kernels, call(): pl.pallas_call(kernel, out_shape=outs, in_specs=specs, scratch_shapes=scr...  10.8 us
    ppermute x3, starting transfers between devices, sent(): lax.ppermute(value, ('core', 'tm'), [(core * blocks + i, core * blocks +...  8.82 us
    all_to_all x3, waiting for transfers between devices, exchanged(): lax.all_to_all(pieces, ALL, split_axis=0, concat_axis=0, tiled=True, axis...  2.93 us
  transfers between devices with their start and end apart: 6, of which 2 were waited for; matrix products, arithmetic and copies ran while one was open for 0% of the time, Pallas kernels for 11%

profile of v7, /device:TPU:1, one launch (start us, length us, event | category | flops | bytes accessed | tf_op | source)
XLA Modules:
  0.0 54.3 jit_solution(2464591299493638697)
XLA Ops:
  0.6 4.0 %shard_map.77 = (f32[352,128]{1,0:T(8,128)}, f32[512,256]{1,0:T(8,128)S(1)}, f32[512,256]{1,0:T(8,128)S(1)}, f32[512,256]{1,0:T(8,128)S(1)}, f32[1,2048]{1,0:T(1,128)S(1)}, /*index=5*/f32[200,256]{1,0:T(8,128)S(1)}) custom-call(s32[1]{0:T(128)} %bitcast.place, f32[2048,256]{1,0:T(8,128)} %snaps.3, f32[1,2048]{1,0:T(1,128)} %bitcast.20, ...), custom_call_target="tpu_custom_call" | custom-call | tf_op jit(solution)/shard_map/pallas_call | solution.py:37
  4.7 12.0 %all-to-all-start = ((f32[32,1,1408]{2,1,0:T(1,128)}), f32[32,1,1408]{2,1,0:T(1,128)S(1)}, u32[]{:S(2)}, u32[]{:S(2)}) async-start(f32[32,1,1408]{2,1,0:T(1,128)} %bitcast.4), calls=%async_computation | async-start | bytes 360448 | tf_op jit(solution)/shard_map/all_to_all | solution.py:227
  16.7 0.4 shard_map.83
  17.2 2.2 %collective-permute-start.1 = (f32[208,512]{1,0:T(8,128)S(1)}, f32[208,512]{1,0:T(8,128)S(1)}, u32[]{:S(2)}, u32[]{:S(2)}) collective-permute-start(f32[208,512]{1,0:T(8,128)S(1)} %shard_map.83), channel_id=1, source_target_pairs={{0,1},{1,2},{2,3},{3,0},{4,7},{5,4},{6,5},{7,6},{8,9},{9,10},{10,1... | collective-permute-start | bytes 1277960 | tf_op jit(solution)/shard_map/ppermute | solution.py:241
  19.4 1.7 %all-to-all-done = f32[32,1,1408]{2,1,0:T(1,128)S(1)} async-done(((f32[32,1,1408]{2,1,0:T(1,128)}), f32[32,1,1408]{2,1,0:T(1,128)S(1)}, u32[]{:S(2)}, u32[]{:S(2)}) %all-to-all-start) | async-done | bytes 180256 | tf_op jit(solution)/shard_map/all_to_all | solution.py:227
  21.1 0.7 %shard_map.78 = f32[176,128]{1,0:T(8,128)} custom-call(f32[352,128]{1,0:T(8,128)S(1)} %bitcast.13), custom_call_target="tpu_custom_call" | custom-call | tf_op jit(solution)/shard_map/pallas_call | solution.py:37
  21.7 11.8 %all-to-all-start.1 = ((f32[16,1,1408]{2,1,0:T(1,128)}), f32[16,1,1408]{2,1,0:T(1,128)S(1)}, u32[]{:S(2)}, u32[]{:S(2)}) async-start(f32[16,1,1408]{2,1,0:T(1,128)} %bitcast.6), calls=%async_computation.1 | async-start | bytes 180224 | tf_op jit(solution)/shard_map/all_to_all | solution.py:227
  33.6 0.4 shard_map.81
  34.0 2.9 %collective-permute-start = (f32[208,512]{1,0:T(8,128)S(1)}, f32[208,512]{1,0:T(8,128)S(1)}, u32[]{:S(2)}, u32[]{:S(2)}) collective-permute-start(f32[208,512]{1,0:T(8,128)S(1)} %shard_map.81), channel_id=1, source_target_pairs={{0,3},{1,0},{2,1},{3,2},{4,5},{5,6},{6,7},{7,4},{8,11},{9,8},{10,9... | collective-permute-start | bytes 1277960 | tf_op jit(solution)/shard_map/ppermute | solution.py:241
  36.9 0.4 shard_map.82.own
  37.3 0.0 copy-start
  37.3 0.0 copy-start.1
  37.3 0.0 collective-permute-done.1.arrived
  37.3 0.1 shard_map.84
  37.4 3.8 %collective-permute-start.2 = (f32[208,512]{1,0:T(8,128)S(1)}, f32[208,512]{1,0:T(8,128)S(1)}, u32[]{:S(2)}, u32[]{:S(2)}) collective-permute-start(f32[208,512]{1,0:T(8,128)S(1)} %shard_map.84), channel_id=1, source_target_pairs={{0,1},{1,2},{2,3},{3,0},{4,7},{5,4},{6,5},{7,6},{8,9},{9,10},{10,1... | collective-permute-start | bytes 1277960 | tf_op jit(solution)/shard_map/ppermute | solution.py:241
  41.2 0.0 all-to-all-done.1
  41.2 0.7 %shard_map.79 = f32[352,128]{1,0:T(8,128)} custom-call(f32[176,128]{1,0:T(8,128)S(1)} %bitcast.14), custom_call_target="tpu_custom_call" | custom-call | tf_op jit(solution)/shard_map/pallas_call | solution.py:37
  41.9 7.1 %all-to-all-start.2 = ((f32[32,1,1408]{2,1,0:T(1,128)}), f32[32,1,1408]{2,1,0:T(1,128)S(1)}, u32[]{:S(2)}, u32[]{:S(2)}) async-start(f32[32,1,1408]{2,1,0:T(1,128)} %bitcast.8), calls=%async_computation.2 | async-start | bytes 360448 | tf_op jit(solution)/shard_map/all_to_all | solution.py:227
  49.0 1.6 %shard_map.80.own = f32[208,512]{1,0:T(8,128)S(1)} custom-call(s32[1]{0:T(128)} %bitcast.place, f32[2048,256]{1,0:T(8,128)} %snaps.3, f32[1,2048]{1,0:T(1,128)} %bitcast.21, f32[200,256]{1,0:T(8,128)} %bitcast.19), custom_call_target="tpu_custom_call" | custom-call | tf_op jit(solution)/shard_map/pallas_call | solution.py:37
  50.6 0.0 collective-permute-done.from_right
  50.6 0.0 collective-permute-done.2.from_left
  50.6 0.0 copy-done
  50.6 0.0 copy-done.1
  50.7 1.4 %shard_map.85 = (f32[200,512]{1,0:T(8,128)}, f32[4,200]{1,0:T(4,128)S(1)}) custom-call(f32[208,512]{1,0:T(8,128)S(1)} %shard_map.80.own, f32[208,512]{1,0:T(8,128)S(1)} %collective-permute-done.from_right, f32[208,512]{1,0:T(8,128)S(1)} %collective-permute-done.2.from_left, f32[1,200]{1,0:T(1,128)S(1)} %bitcast.15, f32[200,200]{1,0:T(8,128)S(1)} %copy-done), custom_call_target="tpu_custom_call" | custom-call | tf_op jit(solution)/shard_map/pallas_call | solution.py:37
  52.1 1.2 %all-to-all-done.2 = f32[32,1,1408]{2,1,0:T(1,128)S(1)} async-done(((f32[32,1,1408]{2,1,0:T(1,128)}), f32[32,1,1408]{2,1,0:T(1,128)S(1)}, u32[]{:S(2)}, u32[]{:S(2)}) %all-to-all-start.2) | async-done | bytes 180256 | tf_op jit(solution)/shard_map/all_to_all | solution.py:227
  53.3 0.9 %shard_map.86 = f32[200,200]{1,0:T(8,128)} custom-call(f32[352,128]{1,0:T(8,128)S(1)} %bitcast.12, f32[4,200]{1,0:T(4,128)S(1)} %get-tuple-element.16.rows, f32[1,200]{1,0:T(1,128)S(1)} %bitcast.16), custom_call_target="tpu_custom_call" | custom-call | tf_op jit(solution)/shard_map/pallas_call | solution.py:37
Async XLA Ops:
  4.7 16.4 %all-to-all-start = ((f32[32,1,1408]{2,1,0:T(1,128)}), f32[32,1,1408]{2,1,0:T(1,128)S(1)}, u32[]{:S(2)}, u32[]{:S(2)}) async-start(f32[32,1,1408]{2,1,0:T(1,128)} %bitcast.4), calls=%async_computation | async-start | bytes 360448 | tf_op jit(solution)/shard_map/all_to_all | solution.py:227
  17.2 20.2 %collective-permute-start.1 = (f32[208,512]{1,0:T(8,128)S(1)}, f32[208,512]{1,0:T(8,128)S(1)}, u32[]{:S(2)}, u32[]{:S(2)}) collective-permute-start(f32[208,512]{1,0:T(8,128)S(1)} %shard_map.83), channel_id=1, source_target_pairs={{0,1},{1,2},{2,3},{3,0},{4,7},{5,4},{6,5},{7,6},{8,9},{9,10},{10,1... | collective-permute-start | bytes 1277960 | tf_op jit(solution)/shard_map/ppermute | solution.py:241
  21.7 19.4 %all-to-all-start.1 = ((f32[16,1,1408]{2,1,0:T(1,128)}), f32[16,1,1408]{2,1,0:T(1,128)S(1)}, u32[]{:S(2)}, u32[]{:S(2)}) async-start(f32[16,1,1408]{2,1,0:T(1,128)} %bitcast.6), calls=%async_computation.1 | async-start | bytes 180224 | tf_op jit(solution)/shard_map/all_to_all | solution.py:227
  34.0 16.6 %collective-permute-start = (f32[208,512]{1,0:T(8,128)S(1)}, f32[208,512]{1,0:T(8,128)S(1)}, u32[]{:S(2)}, u32[]{:S(2)}) collective-permute-start(f32[208,512]{1,0:T(8,128)S(1)} %shard_map.81), channel_id=1, source_target_pairs={{0,3},{1,0},{2,1},{3,2},{4,5},{5,6},{6,7},{7,4},{8,11},{9,8},{10,9... | collective-permute-start | bytes 1277960 | tf_op jit(solution)/shard_map/ppermute | solution.py:241
  37.3 13.3 %copy-start = (f32[200,200]{1,0:T(8,128)S(1)}, f32[200,200]{1,0:T(8,128)}, u32[]{:S(2)}) copy-start(f32[200,200]{1,0:T(8,128)} %eigen.1) | copy-start | bytes 480004
  37.3 13.3 %copy-start.1 = (f32[200]{0:T(256)S(1)}, f32[200]{0:T(256)}, u32[]{:S(2)}) copy-start(f32[200]{0:T(256)} %param.10) | copy-start | bytes 2404
  37.4 13.2 %collective-permute-start.2 = (f32[208,512]{1,0:T(8,128)S(1)}, f32[208,512]{1,0:T(8,128)S(1)}, u32[]{:S(2)}, u32[]{:S(2)}) collective-permute-start(f32[208,512]{1,0:T(8,128)S(1)} %shard_map.84), channel_id=1, source_target_pairs={{0,1},{1,2},{2,3},{3,0},{4,7},{5,4},{6,5},{7,6},{8,9},{9,10},{10,1... | collective-permute-start | bytes 1277960 | tf_op jit(solution)/shard_map/ppermute | solution.py:241
  41.9 11.4 %all-to-all-start.2 = ((f32[32,1,1408]{2,1,0:T(1,128)}), f32[32,1,1408]{2,1,0:T(1,128)S(1)}, u32[]{:S(2)}, u32[]{:S(2)}) async-start(f32[32,1,1408]{2,1,0:T(1,128)} %bitcast.8), calls=%async_computation.2 | async-start | bytes 360448 | tf_op jit(solution)/shard_map/all_to_all | solution.py:227

commit v8 on v7

--- a/solution.py
+++ b/solution.py
@@ -25,7 +25,7 @@
     return jax.ShapeDtypeStruct(shape, jnp.float32)
 
 
-def call(kernel, out, *args, smem=0, hbm=(), scratch=()):
+def call(kernel, out, *args, smem=0, hbm=(), hbm_out=(), scratch=()):
     whole = pl.BlockSpec(memory_space=pltpu.VMEM)
     scalar = pl.BlockSpec(memory_space=pltpu.SMEM)
     outs = out if isinstance(out, tuple) else (out,)
@@ -39,7 +39,9 @@
         out_shape=outs,
         in_specs=specs,
         scratch_shapes=scratch,
-        out_specs=[whole] * len(outs),
+        out_specs=[
+            pl.BlockSpec(memory_space=pltpu.HBM) if i in hbm_out else whole for i in range(len(outs))
+        ],
         compiler_params=pltpu.CompilerParams(vmem_limit_bytes=VMEM_GRANT),
     )(*args)
     return result if isinstance(out, tuple) else result[0]
@@ -185,7 +187,7 @@
     out[:rank, :], out[rank:, :] = shares_of(block, snaps_in[...], final_in[...], vectors_in[...])
 
 
-def dmd_kernel(own, from_right, from_left, sing, eigen, out, rows):
+def dmd_kernel(own, from_right, from_left, sing, eigen, out, rows, done, sems):
     rank = out.shape[0]
     scale = turned(sing[...])[:rank]
     total = own[...] + from_right[...] + from_left[...]
@@ -193,7 +195,16 @@
     last = total[rank + BLOCKS :, :rank]
     rows[...] = last
     summed = total[:rank] + three_pass(split(last), split(first), (0, 0))
-    out[...] = three_pass(split(eigen[...]), split(summed * scale), (0, 0))
+    right = split(eigen[...])
+    half = done.shape[1] // 2
+    copies = []
+    for i in range(2):
+        there = pl.ds(i * half, half)
+        done[:, there] = three_pass(right, split(summed[:, i * half : (i + 1) * half] * scale), (0, 0))
+        copies.append(pltpu.make_async_copy(done.at[:, there], out.at[:, there], sems.at[i]))
+        copies[i].start()
+    for copy in copies:
+        copy.wait()
 
 
 def operator_kernel(packed, rows, sing, out):
@@ -316,6 +327,11 @@
         from_left,
         sing,
         eigen_vectors,
+        hbm_out=(0,),
+        scratch=(
+            pltpu.VMEM((rank, 2 * half), jnp.float32),
+            pltpu.SemaphoreType.DMA((2,)),
+        ),
     )
     reduced_operator = call(operator_kernel, f32(rank, rank), tiles, last_rows, sing)
     return reduced_operator, dmd_modes.T

time: 54.7 us -> 54.7 us (level)
  no operation moved by 1% of the time
where the time goes in v8:
time: 54.7 us; the launch traced here: 54.3 us
  starting transfers between devices  39.8 us (73%)
  Pallas kernels  10.8 us (20%)
  waiting for transfers between devices  2.92 us (5%)
  between operations  0.78 us (1%)
    all_to_all x3, starting transfers between devices, exchanged(): lax.all_to_all(pieces, ALL, split_axis=0, concat_axis=0, tiled=True, axis...  31 us
    pallas_call x10, Pallas kernels, call(): pl.pallas_call(kernel, out_shape=outs, in_specs=specs, scratch_shapes=scr...  10.8 us
    ppermute x3, starting transfers between devices, sent(): lax.ppermute(value, ('core', 'tm'), [(core * blocks + i, core * blocks +...  8.82 us
    all_to_all x3, waiting for transfers between devices, exchanged(): lax.all_to_all(pieces, ALL, split_axis=0, concat_axis=0, tiled=True, axis...  2.91 us
  transfers between devices with their start and end apart: 6, of which 2 were waited for; matrix products, arithmetic and copies ran while one was open for 0% of the time, Pallas kernels for 11%

profile of v8, /device:TPU:1, one launch (start us, length us, event | category | flops | bytes accessed | tf_op | source)
XLA Modules:
  0.0 54.3 jit_solution(15336781194634914006)
XLA Ops:
  0.6 4.0 %shard_map.77 = (f32[352,128]{1,0:T(8,128)}, f32[512,256]{1,0:T(8,128)S(1)}, f32[512,256]{1,0:T(8,128)S(1)}, f32[512,256]{1,0:T(8,128)S(1)}, f32[1,2048]{1,0:T(1,128)S(1)}, /*index=5*/f32[200,256]{1,0:T(8,128)S(1)}) custom-call(s32[1]{0:T(128)} %bitcast.place, f32[2048,256]{1,0:T(8,128)} %snaps.3, f32[1,2048]{1,0:T(1,128)} %bitcast.20, ...), custom_call_target="tpu_custom_call" | custom-call | tf_op jit(solution)/shard_map/pallas_call | solution.py:37
  4.7 12.0 %all-to-all-start = ((f32[32,1,1408]{2,1,0:T(1,128)}), f32[32,1,1408]{2,1,0:T(1,128)S(1)}, u32[]{:S(2)}, u32[]{:S(2)}) async-start(f32[32,1,1408]{2,1,0:T(1,128)} %bitcast.4), calls=%async_computation | async-start | bytes 360448 | tf_op jit(solution)/shard_map/all_to_all | solution.py:238
  16.7 0.4 shard_map.83
  17.2 2.2 %collective-permute-start.1 = (f32[208,512]{1,0:T(8,128)S(1)}, f32[208,512]{1,0:T(8,128)S(1)}, u32[]{:S(2)}, u32[]{:S(2)}) collective-permute-start(f32[208,512]{1,0:T(8,128)S(1)} %shard_map.83), channel_id=1, source_target_pairs={{0,1},{1,2},{2,3},{3,0},{4,7},{5,4},{6,5},{7,6},{8,9},{9,10},{10,1... | collective-permute-start | bytes 1277960 | tf_op jit(solution)/shard_map/ppermute | solution.py:252
  19.4 1.7 %all-to-all-done = f32[32,1,1408]{2,1,0:T(1,128)S(1)} async-done(((f32[32,1,1408]{2,1,0:T(1,128)}), f32[32,1,1408]{2,1,0:T(1,128)S(1)}, u32[]{:S(2)}, u32[]{:S(2)}) %all-to-all-start) | async-done | bytes 180256 | tf_op jit(solution)/shard_map/all_to_all | solution.py:238
  21.1 0.7 %shard_map.78 = f32[176,128]{1,0:T(8,128)} custom-call(f32[352,128]{1,0:T(8,128)S(1)} %bitcast.13), custom_call_target="tpu_custom_call" | custom-call | tf_op jit(solution)/shard_map/pallas_call | solution.py:37
  21.7 11.8 %all-to-all-start.1 = ((f32[16,1,1408]{2,1,0:T(1,128)}), f32[16,1,1408]{2,1,0:T(1,128)S(1)}, u32[]{:S(2)}, u32[]{:S(2)}) async-start(f32[16,1,1408]{2,1,0:T(1,128)} %bitcast.6), calls=%async_computation.1 | async-start | bytes 180224 | tf_op jit(solution)/shard_map/all_to_all | solution.py:238
  33.6 0.4 shard_map.81
  34.0 2.9 %collective-permute-start = (f32[208,512]{1,0:T(8,128)S(1)}, f32[208,512]{1,0:T(8,128)S(1)}, u32[]{:S(2)}, u32[]{:S(2)}) collective-permute-start(f32[208,512]{1,0:T(8,128)S(1)} %shard_map.81), channel_id=1, source_target_pairs={{0,3},{1,0},{2,1},{3,2},{4,5},{5,6},{6,7},{7,4},{8,11},{9,8},{10,9... | collective-permute-start | bytes 1277960 | tf_op jit(solution)/shard_map/ppermute | solution.py:252
  36.9 0.4 shard_map.82.own
  37.3 0.0 copy-start
  37.3 0.0 copy-start.1
  37.3 0.0 collective-permute-done.1.arrived
  37.3 0.1 shard_map.84
  37.4 3.8 %collective-permute-start.2 = (f32[208,512]{1,0:T(8,128)S(1)}, f32[208,512]{1,0:T(8,128)S(1)}, u32[]{:S(2)}, u32[]{:S(2)}) collective-permute-start(f32[208,512]{1,0:T(8,128)S(1)} %shard_map.84), channel_id=1, source_target_pairs={{0,1},{1,2},{2,3},{3,0},{4,7},{5,4},{6,5},{7,6},{8,9},{9,10},{10,1... | collective-permute-start | bytes 1277960 | tf_op jit(solution)/shard_map/ppermute | solution.py:252
  41.2 0.0 all-to-all-done.1
  41.2 0.7 %shard_map.79 = f32[352,128]{1,0:T(8,128)} custom-call(f32[176,128]{1,0:T(8,128)S(1)} %bitcast.14), custom_call_target="tpu_custom_call" | custom-call | tf_op jit(solution)/shard_map/pallas_call | solution.py:37
  41.9 7.1 %all-to-all-start.2 = ((f32[32,1,1408]{2,1,0:T(1,128)}), f32[32,1,1408]{2,1,0:T(1,128)S(1)}, u32[]{:S(2)}, u32[]{:S(2)}) async-start(f32[32,1,1408]{2,1,0:T(1,128)} %bitcast.8), calls=%async_computation.2 | async-start | bytes 360448 | tf_op jit(solution)/shard_map/all_to_all | solution.py:238
  49.0 1.6 %shard_map.80.own = f32[208,512]{1,0:T(8,128)S(1)} custom-call(s32[1]{0:T(128)} %bitcast.place, f32[2048,256]{1,0:T(8,128)} %snaps.3, f32[1,2048]{1,0:T(1,128)} %bitcast.21, f32[200,256]{1,0:T(8,128)} %bitcast.19), custom_call_target="tpu_custom_call" | custom-call | tf_op jit(solution)/shard_map/pallas_call | solution.py:37
  50.6 0.0 collective-permute-done.from_right
  50.6 0.0 collective-permute-done.2.from_left
  50.6 0.0 copy-done
  50.6 0.0 copy-done.1
  50.7 1.5 %shard_map.85 = (f32[200,512]{1,0:T(8,128)}, f32[4,200]{1,0:T(4,128)S(1)}) custom-call(f32[208,512]{1,0:T(8,128)S(1)} %shard_map.80.own, f32[208,512]{1,0:T(8,128)S(1)} %collective-permute-done.from_right, f32[208,512]{1,0:T(8,128)S(1)} %collective-permute-done.2.from_left, f32[1,200]{1,0:T(1,128)S(1)} %bitcast.15, f32[200,200]{1,0:T(8,128)S(1)} %copy-done), custom_call_target="tpu_custom_call" | custom-call | tf_op jit(solution)/shard_map/pallas_call | solution.py:37
  52.1 1.2 %all-to-all-done.2 = f32[32,1,1408]{2,1,0:T(1,128)S(1)} async-done(((f32[32,1,1408]{2,1,0:T(1,128)}), f32[32,1,1408]{2,1,0:T(1,128)S(1)}, u32[]{:S(2)}, u32[]{:S(2)}) %all-to-all-start.2) | async-done | bytes 180256 | tf_op jit(solution)/shard_map/all_to_all | solution.py:238
  53.3 0.9 %shard_map.86 = f32[200,200]{1,0:T(8,128)} custom-call(f32[352,128]{1,0:T(8,128)S(1)} %bitcast.12, f32[4,200]{1,0:T(4,128)S(1)} %get-tuple-element.16.rows, f32[1,200]{1,0:T(1,128)S(1)} %bitcast.16), custom_call_target="tpu_custom_call" | custom-call | tf_op jit(solution)/shard_map/pallas_call | solution.py:37
Async XLA Ops:
  4.7 16.4 %all-to-all-start = ((f32[32,1,1408]{2,1,0:T(1,128)}), f32[32,1,1408]{2,1,0:T(1,128)S(1)}, u32[]{:S(2)}, u32[]{:S(2)}) async-start(f32[32,1,1408]{2,1,0:T(1,128)} %bitcast.4), calls=%async_computation | async-start | bytes 360448 | tf_op jit(solution)/shard_map/all_to_all | solution.py:238
  17.2 20.2 %collective-permute-start.1 = (f32[208,512]{1,0:T(8,128)S(1)}, f32[208,512]{1,0:T(8,128)S(1)}, u32[]{:S(2)}, u32[]{:S(2)}) collective-permute-start(f32[208,512]{1,0:T(8,128)S(1)} %shard_map.83), channel_id=1, source_target_pairs={{0,1},{1,2},{2,3},{3,0},{4,7},{5,4},{6,5},{7,6},{8,9},{9,10},{10,1... | collective-permute-start | bytes 1277960 | tf_op jit(solution)/shard_map/ppermute | solution.py:252
  21.7 19.4 %all-to-all-start.1 = ((f32[16,1,1408]{2,1,0:T(1,128)}), f32[16,1,1408]{2,1,0:T(1,128)S(1)}, u32[]{:S(2)}, u32[]{:S(2)}) async-start(f32[16,1,1408]{2,1,0:T(1,128)} %bitcast.6), calls=%async_computation.1 | async-start | bytes 180224 | tf_op jit(solution)/shard_map/all_to_all | solution.py:238
  34.0 16.6 %collective-permute-start = (f32[208,512]{1,0:T(8,128)S(1)}, f32[208,512]{1,0:T(8,128)S(1)}, u32[]{:S(2)}, u32[]{:S(2)}) collective-permute-start(f32[208,512]{1,0:T(8,128)S(1)} %shard_map.81), channel_id=1, source_target_pairs={{0,3},{1,0},{2,1},{3,2},{4,5},{5,6},{6,7},{7,4},{8,11},{9,8},{10,9... | collective-permute-start | bytes 1277960 | tf_op jit(solution)/shard_map/ppermute | solution.py:252
  37.3 13.3 %copy-start = (f32[200,200]{1,0:T(8,128)S(1)}, f32[200,200]{1,0:T(8,128)}, u32[]{:S(2)}) copy-start(f32[200,200]{1,0:T(8,128)} %eigen.1) | copy-start | bytes 480004
  37.3 13.3 %copy-start.1 = (f32[200]{0:T(256)S(1)}, f32[200]{0:T(256)}, u32[]{:S(2)}) copy-start(f32[200]{0:T(256)} %param.10) | copy-start | bytes 2404
  37.4 13.2 %collective-permute-start.2 = (f32[208,512]{1,0:T(8,128)S(1)}, f32[208,512]{1,0:T(8,128)S(1)}, u32[]{:S(2)}, u32[]{:S(2)}) collective-permute-start(f32[208,512]{1,0:T(8,128)S(1)} %shard_map.84), channel_id=1, source_target_pairs={{0,1},{1,2},{2,3},{3,0},{4,7},{5,4},{6,5},{7,6},{8,9},{9,10},{10,1... | collective-permute-start | bytes 1277960 | tf_op jit(solution)/shard_map/ppermute | solution.py:252
  41.9 11.4 %all-to-all-start.2 = ((f32[32,1,1408]{2,1,0:T(1,128)}), f32[32,1,1408]{2,1,0:T(1,128)S(1)}, u32[]{:S(2)}, u32[]{:S(2)}) async-start(f32[32,1,1408]{2,1,0:T(1,128)} %bitcast.8), calls=%async_computation.2 | async-start | bytes 360448 | tf_op jit(solution)/shard_map/all_to_all | solution.py:238
